TPU v7x, 32 devices: a whole 2x2x4 slice. The times are simulated.
32 devices in a mesh: grp: 4 (over y, x), col: 8 (over z, core).
Axes of the slice: x: 2, y: 2, z: 4, core: 2. Of those that a mesh axis runs over, the one named last changes fastest.
Arguments:
- start_block: float32 [16, 8192], P(None, ('grp', 'col')), may hold values from -6 to 6
- tile_values: float32 [4, 8, 32, 256, 256], P('grp', 'col'), may hold values from 0 to 1, as said below
- tile_row: int32 [4, 8, 32], P('grp', 'col'), may hold values from 0 to 31, as said below
- tile_col: int32 [4, 8, 32], P('grp', 'col'), may hold values from 0 to 31, as said below
- tile_count: int32 [4, 8], P('grp', 'col'), may hold values from 8 to 32, as said below
Outputs:
- basis: float32 [5, 16, 8192], P(None, None, ('grp', 'col'))
- projections: float32 [4, 4, 16, 16], replicated
- factors: float32 [5, 16, 16], replicated
Inputs may be any that keep to these rules, and one draw needn't show every extreme that they name: `tile_row`: A tile of the device at grp index g lies in tile rows g * 8 * 1 to (g + 1) * 8 - 1. `tile_col`: A tile column t of the device at col index c has (t) % 8 == c. Coordinate pairs may repeat; repeated tiles add. The live tiles of a device are its first tile_count slots; some device has all 32 slots live. `tile_values`: entries are nonnegative.
All inputs are finite; a program needn't handle non-finite values.
Results may differ from a plain program's by a relative error of at most 0.0003.
Values sent between devices are 32-bit elements; how exact they have to be, the bound alone decides.
A program may use at most 64 MiB of HBM per device.

v0:
```python
import functools

import jax
import jax.numpy as jnp
from jax import lax
from jax.experimental import pallas as pl
from jax.experimental.pallas import tpu as pltpu
from jax.sharding import PartitionSpec as P

ITERS = 4
HIGHEST = lax.Precision.HIGHEST
MESH = pl.DeviceIdType.MESH
F32 = jnp.float32
BF16 = jnp.bfloat16
LANES = 128


def dot_nt(left, right, precision=None):
    dims = (((1,), (1,)), ((), ()))
    return lax.dot_general(left, right, dims, precision=precision, preferred_element_type=F32)


def dot_nn(left, right, precision=None):
    dims = (((1,), (0,)), ((), ()))
    return lax.dot_general(left, right, dims, precision=precision, preferred_element_type=F32)


def split_two(value):
    high = value.astype(BF16)
    low = (value - high.astype(F32)).astype(BF16)
    return high, low


def factorize(gram):
    width = gram.shape[0]
    row = lax.broadcasted_iota(jnp.int32, gram.shape, 0)
    lane = lax.broadcasted_iota(jnp.int32, gram.shape, 1)
    unit = jnp.where(lane == row + width, 1.0, 0.0).astype(F32)
    work = jnp.where(lane < width, gram, unit)
    for j in range(width):
        column = jnp.broadcast_to(work[:, j : j + 1], work.shape)
        pivot_row = jnp.broadcast_to(work[j : j + 1, :], work.shape)
        pivot = jnp.broadcast_to(column[j : j + 1, :], work.shape)
        scale = jnp.where(row > j, column / pivot, 0.0)
        work = work - scale * pivot_row
    diagonal = jnp.sum(jnp.where(lane == row, work, 0.0), axis=1, keepdims=True)
    work = work / jnp.sqrt(diagonal)
    upper = jnp.where((lane < width) & (lane >= row), work, 0.0)
    identity = jnp.where(lane == row, 1.0, 0.0).astype(F32)
    factor = dot_nt(identity, jnp.concatenate([upper] * (LANES // width), axis=0), HIGHEST)
    return factor[:, :width], work[:, width : 2 * width]


def kernel(
    grp_size, col_size, node_total,
    start_ref, tiles_ref, row_ref, col_ref, count_ref,
    basis_ref, proj_ref, factors_ref,
    raw, high, low, q_ref, row_panel, col_panel, row_split, col_split,
    acc_row, acc_col, got_row, got_col, deg_row, deg_col, deg_got_row, deg_got_col,
    degree_ref, r_ref, one_col, one_grp, two_col, two_grp,
    tile_sem, gather_row_sem, gather_col_sem, scatter_row_sem, scatter_col_sem,
    deg_row_sem, deg_col_sem,
    one_col_sem, one_grp_sem, two_col_sem, two_grp_sem,
):
    grp = lax.axis_index("grp")
    col = lax.axis_index("col")
    slots, tile_size = raw.shape[0], raw.shape[1]
    width = start_ref.shape[0]
    group = 4 if slots % 4 == 0 else 1

    def load_tile(s):
        return pltpu.make_async_copy(tiles_ref.at[s], raw.at[s], tile_sem.at[s])

    def start_load(s, carry):
        load_tile(s).start()
        return carry

    lax.fori_loop(0, slots, start_load, 0)

    barrier = pltpu.get_barrier_semaphore()

    def greet_col(d, carry):
        pl.semaphore_signal(
            barrier, inc=1, device_id=(grp, lax.rem(col + d, col_size)), device_id_type=MESH
        )
        return carry

    def greet_grp(d, carry):
        pl.semaphore_signal(
            barrier, inc=1, device_id=(lax.rem(grp + d, grp_size), col), device_id_type=MESH
        )
        return carry

    lax.fori_loop(1, col_size, greet_col, 0)
    lax.fori_loop(1, grp_size, greet_grp, 0)

    def exchange(axis, source, target, sems, start):
        size = col_size if axis == "col" else grp_size
        me = col if axis == "col" else grp

        def visit(d, carry):
            peer = lax.rem(me + d, size)
            copy = pltpu.make_async_remote_copy(
                src_ref=source(peer),
                dst_ref=target,
                send_sem=sems.at[0, d],
                recv_sem=sems.at[1, d],
                device_id=(grp, peer) if axis == "col" else (peer, col),
                device_id_type=MESH,
            )
            if start:
                copy.start()
            else:
                copy.wait()
            return carry

        lax.fori_loop(1, size, visit, 0, unroll=size <= 8)

    def reduce_start(part, col_buf, col_sems):
        col_buf[col] = part
        exchange("col", lambda peer: col_buf.at[col], col_buf.at[col], col_sems, True)

    def reduce_turn(col_buf, grp_buf, col_sems, grp_sems):
        exchange("col", lambda peer: col_buf.at[col], col_buf.at[col], col_sems, False)
        grp_buf[grp] = jnp.sum(col_buf[...], axis=0)
        exchange("grp", lambda peer: grp_buf.at[grp], grp_buf.at[grp], grp_sems, True)

    def reduce_end(grp_buf, grp_sems):
        exchange("grp", lambda peer: grp_buf.at[grp], grp_buf.at[grp], grp_sems, False)
        return jnp.sum(grp_buf[...], axis=0) / node_total

    def gram_part(block):
        return dot_nt(block, jnp.concatenate([block] * (LANES // width), axis=0), HIGHEST)

    def scatter(rows, cols, row_in, col_in, row_sems, col_sems, start):
        exchange("col", lambda peer: rows.at[peer], row_in.at[col], row_sems, start)
        exchange("grp", lambda peer: cols.at[peer], col_in.at[grp], col_sems, start)

    def total_of(rows, cols, row_in, col_in):
        row_in[col] = rows[col]
        col_in[grp] = cols[grp]
        return jnp.sum(row_in[...], axis=0) + jnp.sum(col_in[...], axis=0)

    def gather(start):
        exchange("col", lambda peer: r_ref, row_panel.at[col], gather_row_sem, start)
        exchange("grp", lambda peer: r_ref, col_panel.at[grp], gather_col_sem, start)

    def add_tiles(pieces_of, sum_rows, sum_cols):
        sum_rows[...] = jnp.zeros_like(sum_rows)
        sum_cols[...] = jnp.zeros_like(sum_cols)

        def visit(n, carry):
            rows, cols, into_rows, into_cols, lives = [], [], [], [], []
            for u in range(group):
                s = n * group + u
                r = jnp.clip(row_ref[s] - grp * col_size, 0, col_size - 1)
                c = jnp.clip(lax.div(col_ref[s], col_size), 0, grp_size - 1)
                into_row, into_col = pieces_of(s, r, c)
                rows.append(r)
                cols.append(c)
                lives.append(jnp.where(s < count_ref[0], 1.0, 0.0).astype(F32))
                into_rows.append(into_row)
                into_cols.append(into_col)
            for size, acc, places, pieces in (
                (col_size, sum_rows, rows, into_rows),
                (grp_size, sum_cols, cols, into_cols),
            ):
                for place in range(size):
                    total = acc[place]
                    for u in range(group):
                        total = total + jnp.where(places[u] == place, lives[u], 0.0) * pieces[u]
                    acc[place] = total
            return carry

        lax.fori_loop(0, slots // group, visit, 0)

    ones = jnp.ones((width, tile_size), BF16)

    def degree_pieces(s, r, c):
        load_tile(s).wait()
        first, second = split_two(raw[s])
        high[s] = first
        low[s] = second
        into_row = dot_nt(ones, first) + dot_nt(ones, second)
        into_col = dot_nn(ones, first) + dot_nn(ones, second)
        return into_row, into_col

    def product_pieces(s, r, c):
        first, second = high[s], low[s]
        at_col, at_row = col_split[c], row_split[r]
        into_row = dot_nt(at_col, first)
        into_row = into_row[:width] + into_row[width:] + dot_nt(at_col[:width], second)
        into_col = dot_nn(at_row, first)
        into_col = into_col[:width] + into_col[width:] + dot_nn(at_row[:width], second)
        return into_row, into_col

    degree_refs = (deg_row, deg_col, deg_got_row, deg_got_col)
    product_refs = (acc_row, acc_col, got_row, got_col)
    degree_sems = (deg_row_sem, deg_col_sem)
    product_sems = (scatter_row_sem, scatter_col_sem)

    def next_block(k, gram):
        factor, inverse = factorize(gram)
        factors_ref[k] = factor
        q_ref[k] = dot_nn(inverse, r_ref[...], HIGHEST)
        return inverse

    q_ref[...] = jnp.zeros_like(q_ref)
    proj_ref[...] = jnp.zeros_like(proj_ref)
    r_ref[...] = start_ref[...]
    start_part = gram_part(start_ref[...])
    pl.semaphore_wait(barrier, col_size + grp_size - 2)
    reduce_start(start_part, two_col, two_col_sem)
    gather(True)
    add_tiles(degree_pieces, deg_row, deg_col)
    scatter(*degree_refs, *degree_sems, True)

    def step(k, carry):
        newest = r_ref[...]
        row_panel[col] = newest
        col_panel[grp] = newest
        gather(False)
        for size, panel, halves in (
            (grp_size, col_panel, col_split),
            (col_size, row_panel, row_split),
        ):
            for place in range(size):
                first, second = split_two(panel[place])
                halves[place, :width] = first
                halves[place, width:] = second
        reduce_turn(two_col, two_grp, two_col_sem, two_grp_sem)
        add_tiles(product_pieces, acc_row, acc_col)
        scatter(*product_refs, *product_sems, True)

        @pl.when(k == 0)
        def _():
            scatter(*degree_refs, *degree_sems, False)
            degree_ref[...] = total_of(*degree_refs)

        inverse = next_block(k, reduce_end(two_grp, two_grp_sem))
        scatter(*product_refs, *product_sems, False)
        laplace = degree_ref[...] * newest - total_of(*product_refs)
        applied = dot_nn(inverse, laplace, HIGHEST)
        stacked = q_ref[...].reshape(-1, tile_size)
        reduce_start(dot_nt(applied, stacked, HIGHEST), one_col, one_col_sem)
        reduce_turn(one_col, one_grp, one_col_sem, one_grp_sem)
        coeffs = reduce_end(one_grp, one_grp_sem)
        residual = applied - dot_nn(coeffs, stacked, HIGHEST)
        r_ref[...] = residual

        @pl.when(k < ITERS - 1)
        def _():
            gather(True)

        reduce_start(gram_part(residual), two_col, two_col_sem)
        for j in range(ITERS):
            proj_ref[k, j] = coeffs[:, j * width : (j + 1) * width]
        return carry

    lax.fori_loop(0, ITERS, step, 0)
    reduce_turn(two_col, two_grp, two_col_sem, two_grp_sem)
    next_block(ITERS, reduce_end(two_grp, two_grp_sem))
    basis_ref[...] = q_ref[: ITERS + 1]


def solution(mesh):
    grp_size, col_size = mesh.shape["grp"], mesh.shape["col"]

    def body(start_block, tile_values, tile_row, tile_col, tile_count):
        width, shard_len = start_block.shape
        slots, tile_size = tile_values.shape[2], tile_values.shape[3]
        assert shard_len == tile_size and LANES % width == 0
        places = LANES // width
        node_total = shard_len * grp_size * col_size
        vmem = pl.BlockSpec(memory_space=pltpu.VMEM)
        smem = pl.BlockSpec(memory_space=pltpu.SMEM)
        block = (width, tile_size)
        small = (width, LANES)

        def sems(size):
            return pltpu.SemaphoreType.DMA((2, size))

        return pl.pallas_call(
            functools.partial(kernel, grp_size, col_size, node_total),
            out_shape=(
                jax.ShapeDtypeStruct((ITERS + 1,) + block, F32),
                jax.ShapeDtypeStruct((ITERS, ITERS, width, width), F32),
                jax.ShapeDtypeStruct((ITERS + 1, width, width), F32),
            ),
            in_specs=[vmem, pl.BlockSpec(memory_space=pl.ANY), smem, smem, smem],
            out_specs=(vmem, vmem, vmem),
            scratch_shapes=[
                pltpu.VMEM((slots, tile_size, tile_size), F32),
                pltpu.VMEM((slots, tile_size, tile_size), BF16),
                pltpu.VMEM((slots, tile_size, tile_size), BF16),
                pltpu.VMEM((places,) + block, F32),
                pltpu.VMEM((col_size,) + block, F32),
                pltpu.VMEM((grp_size,) + block, F32),
                pltpu.VMEM((col_size, 2 * width, tile_size), BF16),
                pltpu.VMEM((grp_size, 2 * width, tile_size), BF16),
                pltpu.VMEM((col_size,) + block, F32),
                pltpu.VMEM((grp_size,) + block, F32),
                pltpu.VMEM((col_size,) + block, F32),
                pltpu.VMEM((grp_size,) + block, F32),
                pltpu.VMEM((col_size,) + block, F32),
                pltpu.VMEM((grp_size,) + block, F32),
                pltpu.VMEM((col_size,) + block, F32),
                pltpu.VMEM((grp_size,) + block, F32),
                pltpu.VMEM(block, F32),
                pltpu.VMEM(block, F32),
                pltpu.VMEM((col_size,) + small, F32),
                pltpu.VMEM((grp_size,) + small, F32),
                pltpu.VMEM((col_size,) + small, F32),
                pltpu.VMEM((grp_size,) + small, F32),
                pltpu.SemaphoreType.DMA((slots,)),
                sems(col_size), sems(grp_size), sems(col_size), sems(grp_size),
                sems(col_size), sems(grp_size),
                sems(col_size), sems(grp_size), sems(col_size), sems(grp_size),
            ],
            compiler_params=pltpu.CompilerParams(
                collective_id=0, has_side_effects=True, vmem_limit_bytes=40 * 1024 * 1024
            ),
        )(
            start_block,
            tile_values.reshape(slots, tile_size, tile_size),
            tile_row.reshape(slots),
            tile_col.reshape(slots),
            tile_count.reshape(1),
        )

    in_specs = (
        P(None, ("grp", "col")),
        P("grp", "col", None, None, None),
        P("grp", "col", None),
        P("grp", "col", None),
        P("grp", "col"),
    )
    out_specs = (P(None, None, ("grp", "col")), P(), P())
    return jax.shard_map(body, mesh=mesh, in_specs=in_specs, out_specs=out_specs, check_vma=False)
```

profile of v0, /device:TPU:0, one launch (start us, length us, event | category | flops | bytes accessed | tf_op | source)
XLA Modules:
  0.0 115.6 jit_solution(3807898196832445446)
XLA Ops:
  1.3 0.0 copy-start
  1.3 3.4 %copy-done = f32[1,1,32,256,256]{4,3,2,1,0:T(8,128)S(1)} copy-done((f32[1,1,32,256,256]{4,3,2,1,0:T(8,128)S(1)}, f32[1,1,32,256,256]{4,3,2,1,0:T(8,128)}, u32[]{:S(2)}) %copy-start) | copy-done | bytes 8388632
  4.7 0.0 copy-start.1
  4.7 0.7 copy-done.1
  5.4 0.0 copy-start.2
  5.4 0.7 copy-done.2
  6.0 0.0 copy-start.3
  6.0 0.7 copy-done.3
  6.7 107.0 %shard_map.76 = (f32[5,16,256]{2,1,0:T(8,128)S(1)}, f32[4,4,16,16]{3,2,1,0:T(8,128)S(1)}, f32[5,16,16]{2,1,0:T(8,128)S(1)}) custom-call(f32[16,256]{1,0:T(8,128)S(1)} %copy-done.1, f32[32,256,256]{2,1,0:T(8,128)S(1)} %bitcast.5, s32[32]{0:T(128)S(1)} %bitcast.6, s32[32]{0:T(128)S(1)} %bitcast.7, s32[1]{0:T(128)} %bitcast.4.count_ref), custom_call_target="tpu_custom_call" | custom-call | tf_op jit(solution)/shard_map/pallas_call | solution.py:283
  113.7 0.6 copy.12
  114.3 0.7 copy.13
  115.0 0.6 copy.14
Async XLA Ops:
  1.3 3.4 %copy-start = (f32[1,1,32,256,256]{4,3,2,1,0:T(8,128)S(1)}, f32[1,1,32,256,256]{4,3,2,1,0:T(8,128)}, u32[]{:S(2)}) copy-start(f32[1,1,32,256,256]{4,3,2,1,0:T(8,128)} %param.6) | copy-start | bytes 25165828
  4.7 0.7 copy-start.1
  5.4 0.7 copy-start.2
  6.0 0.7 copy-start.3
where the time goes:
time: 116 us
  Pallas kernels  107 us (92%)
  local copies, waits for them, and re-layouts  7.31 us (6%)
  between operations  1.3 us (1%)
    pallas_call x1, Pallas kernels, body(): pl.pallas_call(functools.partial(kernel, grp_size, col_size, node_total),...  107 us
    unnamed x11, local copies, waits for them, and re-layouts  7.31 us

commit v1 on v0

v1 whole, which is shorter than its diff:
```python
import functools

import jax
import jax.numpy as jnp
from jax import lax
from jax.experimental import pallas as pl
from jax.experimental.pallas import tpu as pltpu
from jax.sharding import PartitionSpec as P

ITERS = 4
HIGHEST = lax.Precision.HIGHEST
MESH = pl.DeviceIdType.MESH
F32 = jnp.float32
BF16 = jnp.bfloat16
I32 = jnp.int32
LANES = 128
CHUNK = 8


def dot_nt(left, right, precision=None):
    dims = (((1,), (1,)), ((), ()))
    return lax.dot_general(left, right, dims, precision=precision, preferred_element_type=F32)


def dot_nn(left, right, precision=None):
    dims = (((1,), (0,)), ((), ()))
    return lax.dot_general(left, right, dims, precision=precision, preferred_element_type=F32)


def split_two(value):
    high = value.astype(BF16)
    low = (value - high.astype(F32)).astype(BF16)
    return high, low


def factorize(gram):
    width = gram.shape[0]
    row = lax.broadcasted_iota(I32, gram.shape, 0)
    lane = lax.broadcasted_iota(I32, gram.shape, 1)
    unit = jnp.where(lane == row, 1.0, 0.0).astype(F32)
    work = jnp.where((lane >= width) & (lane < 2 * width), gram, unit)
    for j in range(width):
        column = jnp.broadcast_to(work[:, width + j : width + j + 1], work.shape)
        pivot_row = jnp.broadcast_to(work[j : j + 1, :], work.shape)
        pivot = jnp.broadcast_to(column[j : j + 1, :], work.shape)
        scale = jnp.where(row > j, column / pivot, 0.0)
        work = work - scale * pivot_row
    diagonal = jnp.sum(jnp.where(lane == row + width, work, 0.0), axis=1, keepdims=True)
    work = work / jnp.sqrt(diagonal)
    upper = jnp.where((lane < 2 * width) & (lane >= row + width), work, 0.0)
    inverse = jnp.where(lane <= row, work, 0.0)
    return upper, inverse


def factor_of(upper):
    width = upper.shape[0]
    return upper[:, width : 2 * width].T


def far_first(size):
    return sorted(range(1, size), key=lambda d: (-min(d, size - d), d)) + [0]


def kernel(
    grp_size, col_size, node_total,
    start_ref, tiles_ref, row_ref, col_ref, count_ref,
    basis_ref, proj_ref, factors_ref,
    raw, merged, high, low, rows_v, cols_v, table_v, table,
    u_ref, lr_ref, stack, lstack, row_panel, col_panel, row_split, col_split,
    acc_row, acc_col, got_row, got_col, deg_row, deg_col, deg_got_row, deg_got_col,
    degree_ref, sigma_ref, coeff_ref, red_col, red_grp, end_col, end_grp,
    tile_sem, in_sem, gather_row_sem, gather_col_sem, scatter_row_sem, scatter_col_sem,
    deg_row_sem, deg_col_sem, red_col_sem, red_grp_sem, end_col_sem, end_grp_sem,
):
    grp = lax.axis_index("grp")
    col = lax.axis_index("col")
    slots, tile_size = raw.shape[0], raw.shape[1]
    width = u_ref.shape[1]
    small = (width, LANES)
    row = lax.broadcasted_iota(I32, small, 0)
    lane = lax.broadcasted_iota(I32, small, 1)

    def load_tile(s):
        return pltpu.make_async_copy(tiles_ref.at[s], raw.at[s], tile_sem.at[s])

    loads = (
        pltpu.make_async_copy(start_ref, u_ref.at[0], in_sem.at[0]),
        pltpu.make_async_copy(row_ref, rows_v, in_sem.at[1]),
        pltpu.make_async_copy(col_ref, cols_v, in_sem.at[2]),
    )
    for copy in loads:
        copy.start()

    def start_load(s, carry):
        load_tile(s).start()
        return carry

    lax.fori_loop(0, slots, start_load, 0)

    barrier = pltpu.get_barrier_semaphore()

    def greet_col(d, carry):
        pl.semaphore_signal(
            barrier, inc=1, device_id=(grp, lax.rem(col + d, col_size)), device_id_type=MESH
        )
        return carry

    def greet_grp(d, carry):
        pl.semaphore_signal(
            barrier, inc=1, device_id=(lax.rem(grp + d, grp_size), col), device_id_type=MESH
        )
        return carry

    lax.fori_loop(1, col_size, greet_col, 0)
    lax.fori_loop(1, grp_size, greet_grp, 0)

    def copy_to(axis, d, source, target, sems):
        size = col_size if axis == "col" else grp_size
        peer = lax.rem((col if axis == "col" else grp) + d, size)
        return pltpu.make_async_remote_copy(
            src_ref=source(peer),
            dst_ref=target,
            send_sem=sems.at[0, d],
            recv_sem=sems.at[1, d],
            device_id=(grp, peer) if axis == "col" else (peer, col),
            device_id_type=MESH,
        )

    def exchange(axis, source, target, sems, start):
        size = col_size if axis == "col" else grp_size

        def visit(d, carry):
            copy = copy_to(axis, d, source, target, sems)
            if start:
                copy.start()
            else:
                copy.wait()
            return carry

        lax.fori_loop(1, size, visit, 0, unroll=size <= 8)

    def gather_col(par, start):
        exchange("grp", lambda peer: u_ref.at[par], col_panel.at[par, grp], gather_col_sem.at[par], start)

    def gather_row(par, start):
        exchange("col", lambda peer: u_ref.at[par], row_panel.at[par, col], gather_row_sem.at[par], start)

    def spread(axis, buf, sems, start):
        me = col if axis == "col" else grp
        exchange(axis, lambda peer: buf.at[me], buf.at[me], sems, start)

    def position(r, q):
        return table[0, r * grp_size + q]

    def send_rows(par, r, d, with_degree):
        copy_to("col", d, lambda peer: acc_row.at[r], got_row.at[par, col], scatter_row_sem.at[par]).start()
        if with_degree:
            copy_to("col", d, lambda peer: deg_row.at[r], deg_got_row.at[col], deg_row_sem).start()

    def halves(panel, par, size, split, with_degree):
        for place in range(size):
            first, second = split_two(panel[par, place])
            at = pl.ds(place * tile_size, tile_size)
            split[:width, at] = first
            split[width : 2 * width, at] = second
            if with_degree:
                split[2 * width :, at] = jnp.ones((width, tile_size), BF16)

    def rows_of(r, with_degree):
        left = col_split[...] if with_degree else col_split[: 2 * width]
        firsts = jnp.concatenate([high[position(r, q)] for q in range(grp_size)], axis=1)
        seconds = jnp.concatenate([low[position(r, q)] for q in range(grp_size)], axis=1)
        total = dot_nt(left, firsts)
        rest = dot_nt(left[:width], seconds)
        piece = total[:width] + total[width : 2 * width] + rest
        if not with_degree:
            return piece, None
        return piece, total[2 * width : 2 * width + 1] + dot_nt(left[2 * width :], seconds)[:1]

    def cols_of(q, with_degree):
        piece, degree = 0.0, 0.0
        chunk = CHUNK if col_size % CHUNK == 0 else 1
        for base in range(0, col_size, chunk):
            at = pl.ds(base * tile_size, chunk * tile_size)
            left = row_split[:, at] if with_degree else row_split[: 2 * width, at]
            places = [position(base + r, q) for r in range(chunk)]
            firsts = jnp.concatenate([high[p] for p in places], axis=0)
            seconds = jnp.concatenate([low[p] for p in places], axis=0)
            total = dot_nn(left, firsts)
            rest = dot_nn(left[:width], seconds)
            piece = piece + total[:width] + total[width : 2 * width] + rest
            if with_degree:
                extra = dot_nn(left[2 * width :], seconds)
                degree = degree + total[2 * width : 2 * width + 1] + extra[:1]
        return piece, degree

    def all_rows(par, with_degree):
        def visit(d, carry):
            r = lax.rem(col + d, col_size)
            piece, degree = rows_of(r, with_degree)
            acc_row[r] = piece
            if with_degree:
                deg_row[r] = degree
            return carry

        if col_size <= 8:
            order = far_first(col_size)
            for base in range(0, col_size, 4):
                for d in order[base : base + 4]:
                    visit(d, 0)
                for d in order[base : base + 4]:
                    if d:
                        send_rows(par, lax.rem(col + d, col_size), d, with_degree)
        else:
            def go(d, carry):
                visit(d, 0)
                send_rows(par, lax.rem(col + d, col_size), d, with_degree)
                return carry

            lax.fori_loop(1, col_size, go, 0)
            visit(0, 0)
        got_row[par, col] = acc_row[col]
        if with_degree:
            deg_got_row[col] = deg_row[col]

    def all_cols(par, with_degree):
        for d in far_first(grp_size):
            q = lax.rem(grp + d, grp_size)
            piece, degree = cols_of(q, with_degree)
            acc_col[q] = piece
            if with_degree:
                deg_col[q] = degree
        exchange("grp", lambda peer: acc_col.at[peer], got_col.at[par, grp], scatter_col_sem.at[par], True)
        got_col[par, grp] = acc_col[grp]
        if with_degree:
            exchange("grp", lambda peer: deg_col.at[peer], deg_got_col.at[grp], deg_col_sem, True)
            deg_got_col[grp] = deg_col[grp]

    def collect(par, with_degree):
        exchange("col", lambda peer: acc_row.at[peer], got_row.at[par, col], scatter_row_sem.at[par], False)
        exchange("grp", lambda peer: acc_col.at[peer], got_col.at[par, grp], scatter_col_sem.at[par], False)
        if with_degree:
            exchange("col", lambda peer: deg_row.at[peer], deg_got_row.at[col], deg_row_sem, False)
            exchange("grp", lambda peer: deg_col.at[peer], deg_got_col.at[grp], deg_col_sem, False)
            degree_ref[...] = jnp.sum(deg_got_row[...], axis=0) + jnp.sum(deg_got_col[...], axis=0)
        total = jnp.sum(got_row[par], axis=0) + jnp.sum(got_col[par], axis=0)
        return degree_ref[...] * u_ref[par] - total

    loads[0].wait()
    stack[...] = jnp.zeros_like(stack)
    lstack[...] = jnp.zeros_like(lstack)
    start = u_ref[0]
    stack[0] = start
    stack[1] = start
    row_panel[0, col] = start
    col_panel[0, grp] = start
    pl.semaphore_wait(barrier, col_size + grp_size - 2)
    gather_col(0, True)
    gather_row(0, True)

    loads[1].wait()
    loads[2].wait()
    spots = table.shape[1]
    offset = rows_v[...] - grp * col_size
    pick = lax.div(cols_v[...] - col, col_size)
    place = jnp.clip(offset, 0, col_size - 1) * grp_size + jnp.clip(pick, 0, grp_size - 1)
    square = (slots, slots)
    down = lax.broadcasted_iota(I32, square, 0)
    across = lax.broadcasted_iota(I32, square, 1)
    wide = jnp.broadcast_to(place, square)
    tall = jnp.sum(jnp.where(down == across, wide, 0), axis=1, keepdims=True)
    same = (wide == jnp.broadcast_to(tall, square)) & (down < across)
    before = jnp.max(jnp.where(same, down, -1), axis=0, keepdims=True)
    before = jnp.where(before < 0, slots, before)
    long = (slots, spots)
    depth = lax.broadcasted_iota(I32, long, 0)
    spot = lax.broadcasted_iota(I32, long, 1)
    here = (jnp.broadcast_to(tall, long) == spot) & (depth < count_ref[0])
    last = jnp.max(jnp.where(here, depth, -1), axis=0, keepdims=True)
    table_v[0:1, :] = jnp.where(last < 0, slots, last)
    table_v[1:2, :slots] = before
    move = pltpu.make_async_copy(table_v, table, in_sem.at[3])
    move.start()
    empty = jnp.zeros((tile_size, tile_size), F32)
    merged[slots] = empty
    high[slots] = empty.astype(BF16)
    low[slots] = empty.astype(BF16)
    move.wait()

    def merge(s, carry):
        load_tile(s).wait()
        value = raw[s] + merged[table[1, s]]
        merged[s] = value
        first, second = split_two(value)
        high[s] = first
        low[s] = second
        return carry

    lax.fori_loop(0, slots, merge, 0)

    gather_col(0, False)
    halves(col_panel, 0, grp_size, col_split, True)
    all_rows(0, True)
    gather_row(0, False)
    halves(row_panel, 0, col_size, row_split, True)
    all_cols(0, True)
    applied = collect(0, True)
    lr_ref[...] = applied
    u_ref[1] = applied
    sigma_ref[...] = jnp.zeros_like(sigma_ref)

    def settle(total, inverse):
        left = inverse[:, :width]
        fresh = dot_nn(left, jnp.concatenate([stack[1], lr_ref[...]], axis=1), HIGHEST)
        newest, image = fresh[:, :tile_size], fresh[:, tile_size:]
        pad = jnp.concatenate([inverse, jnp.zeros((LANES - width, LANES), F32)], axis=0)
        mixed = dot_nt(total[:, :width], pad[:, :width], HIGHEST)
        coeffs = jnp.where(lane < width, mixed, jnp.where((lane >= 2 * width) & (lane < 5 * width), total, 0.0))
        stack[0] = newest
        lstack[0] = image
        return left, newest, image, coeffs

    def step(k, carry):
        par = lax.rem(k + 1, 2)
        row_panel[par, col] = u_ref[par]
        col_panel[par, grp] = u_ref[par]
        gather_col(par, True)
        gather_row(par, True)
        block = stack[0:4].reshape(4 * width, tile_size)
        block = jnp.concatenate([block, block], axis=0)
        both = dot_nt(jnp.concatenate([u_ref[par], stack[1]], axis=0), block, HIGHEST)
        gram_lanes = (lax.rem(lane, 4 * width) >= width) & (lax.rem(lane, 4 * width) < 2 * width)
        part = jnp.where(gram_lanes, both[width:], both[:width])
        half = width // 2
        red_col[par, col] = jnp.where(lane[:half] < LANES // 2, part[:half], part[half:])
        spread("col", red_col.at[par], red_col_sem.at[par], True)

        gather_col(par, False)
        halves(col_panel, par, grp_size, col_split, False)
        all_rows(par, False)

        spread("col", red_col.at[par], red_col_sem.at[par], False)
        red_grp[par, grp] = jnp.sum(red_col[par], axis=0)
        spread("grp", red_grp.at[par], red_grp_sem.at[par], True)

        gather_row(par, False)
        halves(row_panel, par, col_size, row_split, False)
        all_cols(par, False)

        spread("grp", red_grp.at[par], red_grp_sem.at[par], False)
        packed = jnp.sum(red_grp[par], axis=0) / node_total
        total = jnp.concatenate([packed, pltpu.roll(packed, LANES // 2, 1)], axis=0)
        total = jnp.where(lane < LANES // 2, total, 0.0)
        upper, inverse = factorize(total)
        left, newest, image, coeffs = settle(total, inverse)
        factors_ref[k] = factor_of(upper)
        basis_ref[k] = newest
        now = dot_nn(coeffs, jnp.concatenate([stack[...].reshape(LANES, tile_size),
                                              lstack[...].reshape(LANES, tile_size)], axis=1), HIGHEST)
        residual = dot_nn(left, u_ref[par] - now[:, :tile_size], HIGHEST)
        known = now[:, tile_size:]
        found = dot_nn(left, coeffs, HIGHEST)
        found = found + jnp.where(lane == row, sigma_ref[:, :LANES], 0.0)
        coeff_ref[k] = found
        mean = jnp.sum(jnp.where(lane == row, found, 0.0), axis=1, keepdims=True)
        mean = jnp.sum(mean, axis=0, keepdims=True) / width
        sigma = jnp.where(k == 0, jnp.broadcast_to(mean, sigma_ref.shape), sigma_ref[...])
        stack[k + 2] = newest
        lstack[k + 2] = image
        stack[0] = residual
        stack[1] = residual

        applied = collect(par, False)
        image_next = dot_nn(left, applied - known, HIGHEST)
        lr_ref[...] = image_next
        u_ref[1 - par] = image_next - sigma * residual
        sigma_ref[...] = sigma
        return carry

    lax.fori_loop(0, ITERS - 1, step, 0)

    k = ITERS - 1
    par = ITERS % 2
    block_u = u_ref[par]
    stack[5] = block_u
    both = dot_nt(jnp.concatenate([block_u, stack[1]], axis=0), stack[...].reshape(LANES, tile_size), HIGHEST)
    end_col[col] = jnp.where((lane >= width) & (lane < 2 * width), both[width:], both[:width])
    spread("col", end_col, end_col_sem, True)
    spread("col", end_col, end_col_sem, False)
    end_grp[grp] = jnp.sum(end_col[...], axis=0)
    spread("grp", end_grp, end_grp_sem, True)
    spread("grp", end_grp, end_grp_sem, False)
    total = jnp.sum(end_grp[...], axis=0) / node_total
    upper, inverse = factorize(total)
    left, newest, image, coeffs = settle(total, inverse)
    factors_ref[k] = factor_of(upper)
    basis_ref[k] = newest
    now = dot_nn(coeffs, stack[...].reshape(LANES, tile_size), HIGHEST)
    residual = dot_nn(left, block_u - now, HIGHEST)
    found = dot_nn(left, coeffs, HIGHEST)
    coeff_ref[k] = found + jnp.where(lane == row, sigma_ref[:, :LANES], 0.0)
    inner = total[:, 5 * width : 6 * width] - dot_nt(coeffs, coeffs, HIGHEST)
    outer = dot_nt(dot_nn(left, inner, HIGHEST), left, HIGHEST)
    gram = jnp.concatenate([outer] * (LANES // width), axis=1)
    upper, inverse = factorize(gram)
    factors_ref[ITERS] = factor_of(upper)
    basis_ref[ITERS] = dot_nn(inverse[:, :width], residual, HIGHEST)
    proj_ref[...] = jnp.zeros_like(proj_ref)
    for k in range(ITERS):
        for j in range(k):
            proj_ref[k, j] = coeff_ref[k, :, (j + 2) * width : (j + 3) * width]
        proj_ref[k, k] = coeff_ref[k, :, :width]


def solution(mesh):
    grp_size, col_size = mesh.shape["grp"], mesh.shape["col"]

    def body(start_block, tile_values, tile_row, tile_col, tile_count):
        width, shard_len = start_block.shape
        slots, tile_size = tile_values.shape[2], tile_values.shape[3]
        assert shard_len == tile_size and LANES // width == 8
        places = LANES // width
        node_total = shard_len * grp_size * col_size
        spots = -(-max(grp_size * col_size, slots) // LANES) * LANES
        vmem = pl.BlockSpec(memory_space=pltpu.VMEM)
        smem = pl.BlockSpec(memory_space=pltpu.SMEM)
        hbm = pl.BlockSpec(memory_space=pl.ANY)
        block = (width, tile_size)
        line = (1, tile_size)
        tiles = (slots + 1, tile_size, tile_size)
        packed = (width // 2, LANES)
        small = (width, LANES)

        def sems(*sizes):
            return pltpu.SemaphoreType.DMA(sizes)

        return pl.pallas_call(
            functools.partial(kernel, grp_size, col_size, node_total),
            out_shape=(
                jax.ShapeDtypeStruct((ITERS + 1,) + block, F32),
                jax.ShapeDtypeStruct((ITERS, ITERS, width, width), F32),
                jax.ShapeDtypeStruct((ITERS + 1, width, width), F32),
            ),
            in_specs=[hbm, hbm, hbm, hbm, smem],
            out_specs=(vmem, vmem, vmem),
            scratch_shapes=[
                pltpu.VMEM((slots, tile_size, tile_size), F32),
                pltpu.VMEM(tiles, F32),
                pltpu.VMEM(tiles, BF16),
                pltpu.VMEM(tiles, BF16),
                pltpu.VMEM((1, slots), I32),
                pltpu.VMEM((1, slots), I32),
                pltpu.VMEM((8, spots), I32),
                pltpu.SMEM((8, spots), I32),
                pltpu.VMEM((2,) + block, F32),
                pltpu.VMEM(block, F32),
                pltpu.VMEM((places,) + block, F32),
                pltpu.VMEM((places,) + block, F32),
                pltpu.VMEM((2, col_size) + block, F32),
                pltpu.VMEM((2, grp_size) + block, F32),
                pltpu.VMEM((3 * width, col_size * tile_size), BF16),
                pltpu.VMEM((3 * width, grp_size * tile_size), BF16),
                pltpu.VMEM((col_size,) + block, F32),
                pltpu.VMEM((grp_size,) + block, F32),
                pltpu.VMEM((2, col_size) + block, F32),
                pltpu.VMEM((2, grp_size) + block, F32),
                pltpu.VMEM((col_size,) + line, F32),
                pltpu.VMEM((grp_size,) + line, F32),
                pltpu.VMEM((col_size,) + line, F32),
                pltpu.VMEM((grp_size,) + line, F32),
                pltpu.VMEM(line, F32),
                pltpu.VMEM(block, F32),
                pltpu.VMEM((ITERS,) + small, F32),
                pltpu.VMEM((2, col_size) + packed, F32),
                pltpu.VMEM((2, grp_size) + packed, F32),
                pltpu.VMEM((col_size,) + small, F32),
                pltpu.VMEM((grp_size,) + small, F32),
                sems(slots),
                sems(4),
                sems(2, 2, col_size), sems(2, 2, grp_size),
                sems(2, 2, col_size), sems(2, 2, grp_size),
                sems(2, col_size), sems(2, grp_size),
                sems(2, 2, col_size), sems(2, 2, grp_size),
                sems(2, col_size), sems(2, grp_size),
            ],
            compiler_params=pltpu.CompilerParams(
                collective_id=0, has_side_effects=True, vmem_limit_bytes=60 * 1024 * 1024
            ),
        )(
            start_block,
            tile_values.reshape(slots, tile_size, tile_size),
            tile_row.reshape(1, slots),
            tile_col.reshape(1, slots),
            tile_count.reshape(1),
        )

    in_specs = (
        P(None, ("grp", "col")),
        P("grp", "col", None, None, None),
        P("grp", "col", None),
        P("grp", "col", None),
        P("grp", "col"),
    )
    out_specs = (P(None, None, ("grp", "col")), P(), P())
    return jax.shard_map(body, mesh=mesh, in_specs=in_specs, out_specs=out_specs, check_vma=False)
```

time: 116 us -> 73.4 us (0.63)
  Pallas kernels: 107 us -> 67.3 us
  local copies, waits for them, and re-layouts: 7.31 us -> 4.49 us
    pallas_call x1, Pallas kernels: 107 us -> 67.3 us  [body(): pl.pallas_call(functools.partial(kernel, grp_size, col_size, node_total),...]
    unnamed x11 -> x3, local copies, waits for them, and re-layouts: 7.31 us -> 4.49 us
where the time goes in v1:
time: 73.4 us; the launch traced here: 73.1 us
  Pallas kernels  67.3 us (92%)
  local copies, waits for them, and re-layouts  4.49 us (6%)
  between operations  1.29 us (2%)
    pallas_call x1, Pallas kernels, body(): pl.pallas_call(functools.partial(kernel, grp_size, col_size, node_total),...  67.3 us
    unnamed x3, local copies, waits for them, and re-layouts  4.49 us

profile of v1, /device:TPU:0, one launch (start us, length us, event | category | flops | bytes accessed | tf_op | source)
XLA Modules:
  0.0 73.1 jit_solution(15369190274538006445)
XLA Ops:
  1.3 67.3 %shard_map.76 = (f32[5,16,256]{2,1,0:T(8,128)}, f32[4,4,16,16]{3,2,1,0:T(8,128)}, f32[5,16,16]{2,1,0:T(8,128)}) custom-call(f32[16,256]{1,0:T(8,128)} %start_ref.1, f32[32,256,256]{2,1,0:T(8,128)} %bitcast.5, s32[1,32]{1,0:T(1,128)} %bitcast.6, s32[1,32]{1,0:T(1,128)} %bitcast.7, s32[1]{0:T(128)} %bitcast.4.count_ref), custom_call_target="tpu_custom_call" | custom-call | tf_op jit(solution)/shard_map/pallas_call | solution.py:437
  68.6 1.5 %copy.12 = f32[5,16,256]{2,1,0:T(8,128)} copy(f32[5,16,256]{2,1,0:T(8,128)} %get-tuple-element.6) | data formatting | bytes 163840
  70.1 1.6 %copy.13 = f32[4,4,16,16]{3,2,1,0:T(8,128)} copy(f32[4,4,16,16]{3,2,1,0:T(8,128)} %get-tuple-element.7) | data formatting | bytes 32768
  71.7 1.4 %copy.14 = f32[5,16,16]{2,1,0:T(8,128)} copy(f32[5,16,16]{2,1,0:T(8,128)} %get-tuple-element.8) | data formatting | bytes 10240

commit v2 on v1

--- a/solution.py
+++ b/solution.py
@@ -15,6 +15,7 @@
 I32 = jnp.int32
 LANES = 128
 CHUNK = 8
+STRIDE = 4
 
 
 def dot_nt(left, right, precision=None):
@@ -35,17 +36,31 @@
 
 def factorize(gram):
     width = gram.shape[0]
-    row = lax.broadcasted_iota(I32, gram.shape, 0)
-    lane = lax.broadcasted_iota(I32, gram.shape, 1)
+    shape = gram.shape
+    row = lax.broadcasted_iota(I32, shape, 0)
+    lane = lax.broadcasted_iota(I32, shape, 1)
     unit = jnp.where(lane == row, 1.0, 0.0).astype(F32)
     work = jnp.where((lane >= width) & (lane < 2 * width), gram, unit)
-    for j in range(width):
-        column = jnp.broadcast_to(work[:, width + j : width + j + 1], work.shape)
-        pivot_row = jnp.broadcast_to(work[j : j + 1, :], work.shape)
-        pivot = jnp.broadcast_to(column[j : j + 1, :], work.shape)
-        scale = jnp.where(row > j, column / pivot, 0.0)
-        work = work - scale * pivot_row
-    diagonal = jnp.sum(jnp.where(lane == row + width, work, 0.0), axis=1, keepdims=True)
+    diagonal = jnp.ones(shape, F32)
+    for base in range(0, width, STRIDE):
+        tall = [jnp.broadcast_to(work[:, width + base + i : width + base + i + 1], shape) for i in range(STRIDE)]
+        wide = [jnp.broadcast_to(work[base + i : base + i + 1, :], shape) for i in range(STRIDE)]
+        cell = {
+            (m, i): jnp.broadcast_to(tall[i][base + m : base + m + 1, :], shape)
+            for i in range(STRIDE)
+            for m in range(i, STRIDE)
+        }
+        for i in range(STRIDE):
+            inverse = 1.0 / cell[i, i]
+            diagonal = jnp.where(row == base + i, cell[i, i], diagonal)
+            scale = jnp.where(row > base + i, tall[i] * inverse, 0.0)
+            work = work - scale * wide[i]
+            for m in range(i + 1, STRIDE):
+                ratio = cell[m, i] * inverse
+                wide[m] = wide[m] - ratio * wide[i]
+                tall[m] = tall[m] - scale * cell[m, i]
+                for n in range(m, STRIDE):
+                    cell[n, m] = cell[n, m] - ratio * cell[n, i]
     work = work / jnp.sqrt(diagonal)
     upper = jnp.where((lane < 2 * width) & (lane >= row + width), work, 0.0)
     inverse = jnp.where(lane <= row, work, 0.0)
@@ -65,7 +80,7 @@
     grp_size, col_size, node_total,
     start_ref, tiles_ref, row_ref, col_ref, count_ref,
     basis_ref, proj_ref, factors_ref,
-    raw, merged, high, low, rows_v, cols_v, table_v, table,
+    raw, merged, high, low, high_t, low_t, rows_v, cols_v, table_v, table,
     u_ref, lr_ref, stack, lstack, row_panel, col_panel, row_split, col_split,
     acc_row, acc_col, got_row, got_col, deg_row, deg_col, deg_got_row, deg_got_col,
     degree_ref, sigma_ref, coeff_ref, red_col, red_grp, end_col, end_grp,
@@ -162,20 +177,29 @@
             first, second = split_two(panel[par, place])
             at = pl.ds(place * tile_size, tile_size)
             split[:width, at] = first
-            split[width : 2 * width, at] = second
             if with_degree:
-                split[2 * width :, at] = jnp.ones((width, tile_size), BF16)
+                split[width : 2 * width, at] = jnp.ones((width, tile_size), BF16)
+                split[2 * width :, at] = second
+            else:
+                split[width : 2 * width, at] = second
+
+    def combine(total, rest, with_degree):
+        if not with_degree:
+            return total[:width] + total[width:] + rest, None
+        piece = total[:width] + total[2 * width :] + rest[:width]
+        return piece, total[width : width + 1] + rest[width : width + 1]
 
     def rows_of(r, with_degree):
-        left = col_split[...] if with_degree else col_split[: 2 * width]
-        firsts = jnp.concatenate([high[position(r, q)] for q in range(grp_size)], axis=1)
-        seconds = jnp.concatenate([low[position(r, q)] for q in range(grp_size)], axis=1)
-        total = dot_nt(left, firsts)
-        rest = dot_nt(left[:width], seconds)
-        piece = total[:width] + total[width : 2 * width] + rest
-        if not with_degree:
-            return piece, None
-        return piece, total[2 * width : 2 * width + 1] + dot_nt(left[2 * width :], seconds)[:1]
+        places = [position(r, q) for q in range(grp_size)]
+        if with_degree:
+            left = col_split[...]
+            firsts = jnp.concatenate([high[p] for p in places], axis=1)
+            seconds = jnp.concatenate([low[p] for p in places], axis=1)
+            return combine(dot_nt(left, firsts), dot_nt(left[: 2 * width], seconds), True)
+        left = col_split[: 2 * width]
+        firsts = jnp.concatenate([high_t[p] for p in places], axis=0)
+        seconds = jnp.concatenate([low_t[p] for p in places], axis=0)
+        return combine(dot_nn(left, firsts), dot_nn(left[:width], seconds), False)
 
     def cols_of(q, with_degree):
         piece, degree = 0.0, 0.0
@@ -186,12 +210,11 @@
             places = [position(base + r, q) for r in range(chunk)]
             firsts = jnp.concatenate([high[p] for p in places], axis=0)
             seconds = jnp.concatenate([low[p] for p in places], axis=0)
-            total = dot_nn(left, firsts)
-            rest = dot_nn(left[:width], seconds)
-            piece = piece + total[:width] + total[width : 2 * width] + rest
+            rest = dot_nn(left[: 2 * width] if with_degree else left[:width], seconds)
+            part, extra = combine(dot_nn(left, firsts), rest, with_degree)
+            piece = piece + part
             if with_degree:
-                extra = dot_nn(left[2 * width :], seconds)
-                degree = degree + total[2 * width : 2 * width + 1] + extra[:1]
+                degree = degree + extra
         return piece, degree
 
     def all_rows(par, with_degree):
@@ -285,6 +308,8 @@
     merged[slots] = empty
     high[slots] = empty.astype(BF16)
     low[slots] = empty.astype(BF16)
+    high_t[slots] = empty.astype(BF16)
+    low_t[slots] = empty.astype(BF16)
     move.wait()
 
     def merge(s, carry):
@@ -304,6 +329,13 @@
     gather_row(0, False)
     halves(row_panel, 0, col_size, row_split, True)
     all_cols(0, True)
+
+    def turn(s, carry):
+        high_t[s] = high[s].T
+        low_t[s] = low[s].T
+        return carry
+
+    lax.fori_loop(0, slots, turn, 0, unroll=4)
     applied = collect(0, True)
     lr_ref[...] = applied
     u_ref[1] = applied
@@ -412,6 +444,15 @@
         proj_ref[k, k] = coeff_ref[k, :, :width]
 
 
+def deliver(basis, proj, factors, basis_out, proj_out, factors_out, sem):
+    pairs = ((basis, basis_out), (proj, proj_out), (factors, factors_out))
+    copies = [pltpu.make_async_copy(source, target, sem.at[n]) for n, (source, target) in enumerate(pairs)]
+    for copy in copies:
+        copy.start()
+    for copy in copies:
+        copy.wait()
+
+
 def solution(mesh):
     grp_size, col_size = mesh.shape["grp"], mesh.shape["col"]
 
@@ -434,18 +475,24 @@
         def sems(*sizes):
             return pltpu.SemaphoreType.DMA(sizes)
 
-        return pl.pallas_call(
+        def pinned(value):
+            return pltpu.with_memory_space_constraint(value, pltpu.HBM)
+
+        shapes = (
+            jax.ShapeDtypeStruct((ITERS + 1,) + block, F32),
+            jax.ShapeDtypeStruct((ITERS, ITERS, width, width), F32),
+            jax.ShapeDtypeStruct((ITERS + 1, width, width), F32),
+        )
+        results = pl.pallas_call(
             functools.partial(kernel, grp_size, col_size, node_total),
-            out_shape=(
-                jax.ShapeDtypeStruct((ITERS + 1,) + block, F32),
-                jax.ShapeDtypeStruct((ITERS, ITERS, width, width), F32),
-                jax.ShapeDtypeStruct((ITERS + 1, width, width), F32),
-            ),
+            out_shape=shapes,
             in_specs=[hbm, hbm, hbm, hbm, smem],
             out_specs=(vmem, vmem, vmem),
             scratch_shapes=[
                 pltpu.VMEM((slots, tile_size, tile_size), F32),
                 pltpu.VMEM(tiles, F32),
+                pltpu.VMEM(tiles, BF16),
+                pltpu.VMEM(tiles, BF16),
                 pltpu.VMEM(tiles, BF16),
                 pltpu.VMEM(tiles, BF16),
                 pltpu.VMEM((1, slots), I32),
@@ -484,15 +531,22 @@
                 sems(2, col_size), sems(2, grp_size),
             ],
             compiler_params=pltpu.CompilerParams(
-                collective_id=0, has_side_effects=True, vmem_limit_bytes=60 * 1024 * 1024
+                collective_id=0, has_side_effects=True, vmem_limit_bytes=40 * 1024 * 1024
             ),
         )(
-            start_block,
-            tile_values.reshape(slots, tile_size, tile_size),
-            tile_row.reshape(1, slots),
-            tile_col.reshape(1, slots),
+            pinned(start_block),
+            pinned(tile_values.reshape(slots, tile_size, tile_size)),
+            pinned(tile_row.reshape(1, slots)),
+            pinned(tile_col.reshape(1, slots)),
             tile_count.reshape(1),
         )
+        return pl.pallas_call(
+            deliver,
+            out_shape=shapes,
+            in_specs=[vmem] * 3,
+            out_specs=[hbm] * 3,
+            scratch_shapes=[sems(3)],
+        )(*(pltpu.with_memory_space_constraint(value, pltpu.VMEM) for value in results))
 
     in_specs = (
         P(None, ("grp", "col")),

time: 73.4 us -> 61 us (0.83)
  Pallas kernels: 67.3 us -> 59.4 us
  local copies, waits for them, and re-layouts: 4.49 us -> 0 us
    pallas_call x1, Pallas kernels: 67.3 us -> 58.7 us  [body(): pl.pallas_call(functools.partial(kernel, grp_size, col_size, node_total),...]
    unnamed x3 -> x0, local copies, waits for them, and re-layouts: 4.49 us -> none
where the time goes in v2:
time: 61 us; the launch traced here: 60.7 us
  Pallas kernels  59.4 us (97%)
  between operations  1.29 us (2%)
    pallas_call x1, Pallas kernels, body(): pl.pallas_call(functools.partial(kernel, grp_size, col_size, node_total),...  58.7 us

profile of v2, /device:TPU:0, one launch (start us, length us, event | category | flops | bytes accessed | tf_op | source)
XLA Modules:
  0.0 60.7 jit_solution(16971948568641162385)
XLA Ops:
  1.3 58.7 %shard_map.76 = (f32[5,16,256]{2,1,0:T(8,128)S(1)}, f32[4,4,16,16]{3,2,1,0:T(8,128)S(1)}, f32[5,16,16]{2,1,0:T(8,128)S(1)}) custom-call(f32[16,256]{1,0:T(8,128)} %start_ref.1, f32[32,256,256]{2,1,0:T(8,128)} %bitcast.5, s32[1,32]{1,0:T(1,128)} %bitcast.6, s32[1,32]{1,0:T(1,128)} %bitcast.7, s32[1]{0:T(128)} %bitcast.4.count_ref), custom_call_target="tpu_custom_call" | custom-call | tf_op jit(solution)/shard_map/pallas_call | solution.py:486
  60.0 0.7 %shard_map.77 = (f32[5,16,256]{2,1,0:T(8,128)}, f32[4,4,16,16]{3,2,1,0:T(8,128)}, f32[5,16,16]{2,1,0:T(8,128)}) custom-call(f32[5,16,256]{2,1,0:T(8,128)S(1)} %get-tuple-element.6.basis, f32[4,4,16,16]{3,2,1,0:T(8,128)S(1)} %get-tuple-element.7.proj, f32[5,16,16]{2,1,0:T(8,128)S(1)} %get-tuple-element.8.factors), custom_call_target="tpu_custom_call" | custom-call | tf_op jit(solution)/shard_map/pallas_call | solution.py:543

commit v3 on v2

--- a/solution.py
+++ b/solution.py
@@ -72,8 +72,12 @@
     return upper[:, width : 2 * width].T
 
 
-def far_first(size):
-    return sorted(range(1, size), key=lambda d: (-min(d, size - d), d)) + [0]
+def flip(index, distance, size):
+    total, bit = 0, 1
+    while bit < size:
+        total = total + bit * lax.rem(lax.div(index, bit) + lax.div(distance, bit), 2)
+        bit *= 2
+    return total
 
 
 def kernel(
@@ -83,9 +87,9 @@
     raw, merged, high, low, high_t, low_t, rows_v, cols_v, table_v, table,
     u_ref, lr_ref, stack, lstack, row_panel, col_panel, row_split, col_split,
     acc_row, acc_col, got_row, got_col, deg_row, deg_col, deg_got_row, deg_got_col,
-    degree_ref, sigma_ref, coeff_ref, red_col, red_grp, end_col, end_grp,
+    degree_ref, sigma_ref, coeff_ref, red_col, red_grp, early, late,
     tile_sem, in_sem, gather_row_sem, gather_col_sem, scatter_row_sem, scatter_col_sem,
-    deg_row_sem, deg_col_sem, red_col_sem, red_grp_sem, end_col_sem, end_grp_sem,
+    deg_row_sem, deg_col_sem, red_col_sem, red_grp_sem, early_sem, late_sem,
 ):
     grp = lax.axis_index("grp")
     col = lax.axis_index("col")
@@ -95,8 +99,16 @@
     row = lax.broadcasted_iota(I32, small, 0)
     lane = lax.broadcasted_iota(I32, small, 1)
 
-    def load_tile(s):
-        return pltpu.make_async_copy(tiles_ref.at[s], raw.at[s], tile_sem.at[s])
+    def other(t):
+        dg, dc = lax.div(t, col_size), lax.rem(t, col_size)
+        return flip(grp, dg, grp_size), flip(col, dc, col_size)
+
+    loads_of = tile_sem.shape[0]
+    share = slots // loads_of
+
+    def load_tile(n):
+        at = pl.ds(n * share, share)
+        return pltpu.make_async_copy(tiles_ref.at[at], raw.at[at], tile_sem.at[n])
 
     loads = (
         pltpu.make_async_copy(start_ref, u_ref.at[0], in_sem.at[0]),
@@ -110,59 +122,75 @@
         load_tile(s).start()
         return carry
 
-    lax.fori_loop(0, slots, start_load, 0)
+    lax.fori_loop(0, loads_of, start_load, 0)
 
     barrier = pltpu.get_barrier_semaphore()
 
-    def greet_col(d, carry):
-        pl.semaphore_signal(
-            barrier, inc=1, device_id=(grp, lax.rem(col + d, col_size)), device_id_type=MESH
-        )
+    def greet(t, carry):
+        pl.semaphore_signal(barrier, inc=1, device_id=other(t), device_id_type=MESH)
         return carry
 
-    def greet_grp(d, carry):
-        pl.semaphore_signal(
-            barrier, inc=1, device_id=(lax.rem(grp + d, grp_size), col), device_id_type=MESH
-        )
-        return carry
-
-    lax.fori_loop(1, col_size, greet_col, 0)
-    lax.fori_loop(1, grp_size, greet_grp, 0)
+    everyone = grp_size * col_size
+    lax.fori_loop(1, everyone, greet, 0, unroll=everyone <= 32)
 
     def copy_to(axis, d, source, target, sems):
         size = col_size if axis == "col" else grp_size
-        peer = lax.rem((col if axis == "col" else grp) + d, size)
+        peer = flip(col if axis == "col" else grp, d, size)
         return pltpu.make_async_remote_copy(
             src_ref=source(peer),
             dst_ref=target,
-            send_sem=sems.at[0, d],
-            recv_sem=sems.at[1, d],
+            send_sem=sems.at[0],
+            recv_sem=sems.at[1],
             device_id=(grp, peer) if axis == "col" else (peer, col),
             device_id_type=MESH,
         )
 
-    def exchange(axis, source, target, sems, start):
+    def send(axis, source, target, sems):
         size = col_size if axis == "col" else grp_size
 
         def visit(d, carry):
-            copy = copy_to(axis, d, source, target, sems)
-            if start:
-                copy.start()
-            else:
-                copy.wait()
+            copy_to(axis, size - d, source, target, sems).start()
             return carry
 
         lax.fori_loop(1, size, visit, 0, unroll=size <= 8)
 
+    def await_all(buf, sems):
+        part = buf.at[pl.ds(0, buf.shape[0] - 1)]
+        pltpu.make_async_remote_copy(
+            src_ref=part, dst_ref=part, send_sem=sems.at[0], recv_sem=sems.at[1],
+            device_id=other(1), device_id_type=MESH,
+        ).wait()
+
     def gather_col(par, start):
-        exchange("grp", lambda peer: u_ref.at[par], col_panel.at[par, grp], gather_col_sem.at[par], start)
+        if start:
+            send("grp", lambda peer: u_ref.at[par], col_panel.at[par, grp], gather_col_sem.at[par])
+        else:
+            await_all(col_panel.at[par], gather_col_sem.at[par])
 
     def gather_row(par, start):
-        exchange("col", lambda peer: u_ref.at[par], row_panel.at[par, col], gather_row_sem.at[par], start)
+        if start:
+            send("col", lambda peer: u_ref.at[par], row_panel.at[par, col], gather_row_sem.at[par])
+        else:
+            await_all(row_panel.at[par], gather_row_sem.at[par])
 
     def spread(axis, buf, sems, start):
         me = col if axis == "col" else grp
-        exchange(axis, lambda peer: buf.at[me], buf.at[me], sems, start)
+        if start:
+            send(axis, lambda peer: buf.at[me], buf.at[me], sems)
+        else:
+            await_all(buf, sems)
+
+    def spread_all(buf, sems):
+        me = grp * col_size + col
+
+        def visit(t, carry):
+            pltpu.make_async_remote_copy(
+                src_ref=buf.at[me], dst_ref=buf.at[me], send_sem=sems.at[0], recv_sem=sems.at[1],
+                device_id=other(everyone - t), device_id_type=MESH,
+            ).start()
+            return carry
+
+        lax.fori_loop(1, everyone, visit, 0, unroll=everyone <= 32)
 
     def position(r, q):
         return table[0, r * grp_size + q]
@@ -219,7 +247,7 @@
 
     def all_rows(par, with_degree):
         def visit(d, carry):
-            r = lax.rem(col + d, col_size)
+            r = flip(col, d, col_size)
             piece, degree = rows_of(r, with_degree)
             acc_row[r] = piece
             if with_degree:
@@ -227,17 +255,17 @@
             return carry
 
         if col_size <= 8:
-            order = far_first(col_size)
+            order = list(range(col_size - 1, -1, -1))
             for base in range(0, col_size, 4):
                 for d in order[base : base + 4]:
                     visit(d, 0)
                 for d in order[base : base + 4]:
                     if d:
-                        send_rows(par, lax.rem(col + d, col_size), d, with_degree)
+                        send_rows(par, flip(col, d, col_size), d, with_degree)
         else:
             def go(d, carry):
                 visit(d, 0)
-                send_rows(par, lax.rem(col + d, col_size), d, with_degree)
+                send_rows(par, flip(col, d, col_size), d, with_degree)
                 return carry
 
             lax.fori_loop(1, col_size, go, 0)
@@ -247,24 +275,24 @@
             deg_got_row[col] = deg_row[col]
 
     def all_cols(par, with_degree):
-        for d in far_first(grp_size):
-            q = lax.rem(grp + d, grp_size)
+        for d in range(grp_size - 1, -1, -1):
+            q = flip(grp, d, grp_size)
             piece, degree = cols_of(q, with_degree)
             acc_col[q] = piece
             if with_degree:
                 deg_col[q] = degree
-        exchange("grp", lambda peer: acc_col.at[peer], got_col.at[par, grp], scatter_col_sem.at[par], True)
+        send("grp", lambda peer: acc_col.at[peer], got_col.at[par, grp], scatter_col_sem.at[par])
         got_col[par, grp] = acc_col[grp]
         if with_degree:
-            exchange("grp", lambda peer: deg_col.at[peer], deg_got_col.at[grp], deg_col_sem, True)
+            send("grp", lambda peer: deg_col.at[peer], deg_got_col.at[grp], deg_col_sem)
             deg_got_col[grp] = deg_col[grp]
 
     def collect(par, with_degree):
-        exchange("col", lambda peer: acc_row.at[peer], got_row.at[par, col], scatter_row_sem.at[par], False)
-        exchange("grp", lambda peer: acc_col.at[peer], got_col.at[par, grp], scatter_col_sem.at[par], False)
+        await_all(got_row.at[par], scatter_row_sem.at[par])
+        await_all(got_col.at[par], scatter_col_sem.at[par])
         if with_degree:
-            exchange("col", lambda peer: deg_row.at[peer], deg_got_row.at[col], deg_row_sem, False)
-            exchange("grp", lambda peer: deg_col.at[peer], deg_got_col.at[grp], deg_col_sem, False)
+            await_all(deg_got_row, deg_row_sem)
+            await_all(deg_got_col, deg_col_sem)
             degree_ref[...] = jnp.sum(deg_got_row[...], axis=0) + jnp.sum(deg_got_col[...], axis=0)
         total = jnp.sum(got_row[par], axis=0) + jnp.sum(got_col[par], axis=0)
         return degree_ref[...] * u_ref[par] - total
@@ -277,7 +305,7 @@
     stack[1] = start
     row_panel[0, col] = start
     col_panel[0, grp] = start
-    pl.semaphore_wait(barrier, col_size + grp_size - 2)
+    pl.semaphore_wait(barrier, everyone - 1)
     gather_col(0, True)
     gather_row(0, True)
 
@@ -312,16 +340,18 @@
     low_t[slots] = empty.astype(BF16)
     move.wait()
 
-    def merge(s, carry):
-        load_tile(s).wait()
-        value = raw[s] + merged[table[1, s]]
-        merged[s] = value
-        first, second = split_two(value)
-        high[s] = first
-        low[s] = second
+    def merge(n, carry):
+        load_tile(n).wait()
+        for m in range(share):
+            s = n * share + m
+            value = raw[s] + merged[table[1, s]]
+            merged[s] = value
+            first, second = split_two(value)
+            high[s] = first
+            low[s] = second
         return carry
 
-    lax.fori_loop(0, slots, merge, 0)
+    lax.fori_loop(0, loads_of, merge, 0)
 
     gather_col(0, False)
     halves(col_panel, 0, grp_size, col_split, True)
@@ -340,6 +370,18 @@
     lr_ref[...] = applied
     u_ref[1] = applied
     sigma_ref[...] = jnp.zeros_like(sigma_ref)
+
+    half = width // 2
+
+    def fold(value):
+        return jnp.where(lane[:half] < LANES // 2, value[:half], value[half:])
+
+    def unfold(packed):
+        turned = pltpu.roll(packed, LANES // 2, 1)
+        low_lanes = lane[:half] < LANES // 2
+        return jnp.concatenate(
+            [jnp.where(low_lanes, packed, turned), jnp.where(low_lanes, turned, packed)], axis=0
+        )
 
     def settle(total, inverse):
         left = inverse[:, :width]
@@ -363,8 +405,7 @@
         both = dot_nt(jnp.concatenate([u_ref[par], stack[1]], axis=0), block, HIGHEST)
         gram_lanes = (lax.rem(lane, 4 * width) >= width) & (lax.rem(lane, 4 * width) < 2 * width)
         part = jnp.where(gram_lanes, both[width:], both[:width])
-        half = width // 2
-        red_col[par, col] = jnp.where(lane[:half] < LANES // 2, part[:half], part[half:])
+        red_col[par, col] = fold(part)
         spread("col", red_col.at[par], red_col_sem.at[par], True)
 
         gather_col(par, False)
@@ -380,9 +421,7 @@
         all_cols(par, False)
 
         spread("grp", red_grp.at[par], red_grp_sem.at[par], False)
-        packed = jnp.sum(red_grp[par], axis=0) / node_total
-        total = jnp.concatenate([packed, pltpu.roll(packed, LANES // 2, 1)], axis=0)
-        total = jnp.where(lane < LANES // 2, total, 0.0)
+        total = jnp.where(lane < LANES // 2, unfold(jnp.sum(red_grp[par], axis=0) / node_total), 0.0)
         upper, inverse = factorize(total)
         left, newest, image, coeffs = settle(total, inverse)
         factors_ref[k] = factor_of(upper)
@@ -402,6 +441,13 @@
         stack[0] = residual
         stack[1] = residual
 
+        @pl.when(k == ITERS - 2)
+        def _():
+            shifted = [lstack[j] - sigma * stack[j] for j in (4, 2, 3)]
+            block = jnp.concatenate([shifted[0], residual, shifted[1], shifted[2]] * 2, axis=0)
+            early[grp * col_size + col] = fold(dot_nt(residual, block, HIGHEST))
+            spread_all(early, early_sem)
+
         applied = collect(par, False)
         image_next = dot_nn(left, applied - known, HIGHEST)
         lr_ref[...] = image_next
@@ -413,35 +459,47 @@
 
     k = ITERS - 1
     par = ITERS % 2
-    block_u = u_ref[par]
-    stack[5] = block_u
-    both = dot_nt(jnp.concatenate([block_u, stack[1]], axis=0), stack[...].reshape(LANES, tile_size), HIGHEST)
-    end_col[col] = jnp.where((lane >= width) & (lane < 2 * width), both[width:], both[:width])
-    spread("col", end_col, end_col_sem, True)
-    spread("col", end_col, end_col_sem, False)
-    end_grp[grp] = jnp.sum(end_col[...], axis=0)
-    spread("grp", end_grp, end_grp_sem, True)
-    spread("grp", end_grp, end_grp_sem, False)
-    total = jnp.sum(end_grp[...], axis=0) / node_total
+    quarter = width // 4
+    block_u, block_r = u_ref[par], stack[1]
+    both = dot_nt(block_u, jnp.concatenate([block_r, block_u] * (LANES // (2 * width)), axis=0), HIGHEST)
+    both = fold(both)
+    odd = lax.rem(lax.div(lane[:quarter], 2 * width), 2) == 1
+    late[grp * col_size + col] = jnp.where(odd, both[quarter:], both[:quarter])
+    spread_all(late, late_sem)
+    await_all(early, early_sem)
+    total = unfold(jnp.sum(early[...], axis=0) / node_total)
     upper, inverse = factorize(total)
-    left, newest, image, coeffs = settle(total, inverse)
+    left = inverse[:, :width]
+    newest = dot_nn(left, block_r, HIGHEST)
+    stack[0] = newest
+    basis_ref[k] = newest
     factors_ref[k] = factor_of(upper)
-    basis_ref[k] = newest
-    now = dot_nn(coeffs, stack[...].reshape(LANES, tile_size), HIGHEST)
-    residual = dot_nn(left, block_u - now, HIGHEST)
-    found = dot_nn(left, coeffs, HIGHEST)
-    coeff_ref[k] = found + jnp.where(lane == row, sigma_ref[:, :LANES], 0.0)
-    inner = total[:, 5 * width : 6 * width] - dot_nt(coeffs, coeffs, HIGHEST)
-    outer = dot_nt(dot_nn(left, inner, HIGHEST), left, HIGHEST)
-    gram = jnp.concatenate([outer] * (LANES // width), axis=1)
-    upper, inverse = factorize(gram)
-    factors_ref[ITERS] = factor_of(upper)
-    basis_ref[ITERS] = dot_nn(inverse[:, :width], residual, HIGHEST)
+    older = jnp.where((lane >= 2 * width) & (lane < 5 * width), total, 0.0)
+    pad = jnp.concatenate([inverse, jnp.zeros((LANES - width, LANES), F32)], axis=0)[:, :width]
     proj_ref[...] = jnp.zeros_like(proj_ref)
-    for k in range(ITERS):
+
+    def keep_coeffs(k):
         for j in range(k):
             proj_ref[k, j] = coeff_ref[k, :, (j + 2) * width : (j + 3) * width]
         proj_ref[k, k] = coeff_ref[k, :, :width]
+
+    for n in range(ITERS - 1):
+        keep_coeffs(n)
+    await_all(late, late_sem)
+    packed = jnp.sum(late[...], axis=0) / node_total
+    total = jnp.concatenate(
+        [packed] + [pltpu.roll(packed, LANES - n * 2 * width, 1) for n in range(1, 4)], axis=0
+    )
+    coeffs = dot_nt(total[:, :width], pad, HIGHEST) + older
+    middle = jnp.zeros((width, LANES), F32)
+    beside = jnp.concatenate([middle, coeffs] + [middle] * (LANES // width - 2), axis=0)
+    gram = total - dot_nt(coeffs, beside, HIGHEST)
+    rest = block_u - dot_nn(coeffs, stack[...].reshape(LANES, tile_size), HIGHEST)
+    upper, inverse = factorize(gram)
+    basis_ref[ITERS] = dot_nn(inverse[:, :width], rest, HIGHEST)
+    factors_ref[ITERS] = dot_nt(left, upper[:, width : 2 * width], HIGHEST)
+    coeff_ref[k] = dot_nn(left, coeffs, HIGHEST) + jnp.where(lane == row, sigma_ref[:, :LANES], 0.0)
+    keep_coeffs(k)
 
 
 def deliver(basis, proj, factors, basis_out, proj_out, factors_out, sem):
@@ -460,6 +518,7 @@
         width, shard_len = start_block.shape
         slots, tile_size = tile_values.shape[2], tile_values.shape[3]
         assert shard_len == tile_size and LANES // width == 8
+        assert grp_size & (grp_size - 1) == 0 and col_size & (col_size - 1) == 0
         places = LANES // width
         node_total = shard_len * grp_size * col_size
         spots = -(-max(grp_size * col_size, slots) // LANES) * LANES
@@ -520,15 +579,12 @@
                 pltpu.VMEM((ITERS,) + small, F32),
                 pltpu.VMEM((2, col_size) + packed, F32),
                 pltpu.VMEM((2, grp_size) + packed, F32),
-                pltpu.VMEM((col_size,) + small, F32),
-                pltpu.VMEM((grp_size,) + small, F32),
-                sems(slots),
+                pltpu.VMEM((grp_size * col_size,) + packed, F32),
+                pltpu.VMEM((grp_size * col_size, width // 4, LANES), F32),
+                sems(8 if slots % 8 == 0 else slots),
                 sems(4),
-                sems(2, 2, col_size), sems(2, 2, grp_size),
-                sems(2, 2, col_size), sems(2, 2, grp_size),
-                sems(2, col_size), sems(2, grp_size),
-                sems(2, 2, col_size), sems(2, 2, grp_size),
-                sems(2, col_size), sems(2, grp_size),
+                sems(2, 2), sems(2, 2), sems(2, 2), sems(2, 2),
+                sems(2), sems(2), sems(2, 2), sems(2, 2), sems(2), sems(2),
             ],
             compiler_params=pltpu.CompilerParams(
                 collective_id=0, has_side_effects=True, vmem_limit_bytes=40 * 1024 * 1024

time: 61 us -> 57 us (0.934)
  Pallas kernels: 59.4 us -> 55.4 us
    pallas_call x1, Pallas kernels: 58.7 us -> 54.7 us  [body(): pl.pallas_call(functools.partial(kernel, grp_size, col_size, node_total),...]
where the time goes in v3:
time: 57 us; the launch traced here: 56.7 us
  Pallas kernels  55.4 us (97%)
  between operations  1.29 us (2%)
    pallas_call x1, Pallas kernels, body(): pl.pallas_call(functools.partial(kernel, grp_size, col_size, node_total),...  54.7 us

profile of v3, /device:TPU:0, one launch (start us, length us, event | category | flops | bytes accessed | tf_op | source)
XLA Modules:
  0.0 56.7 jit_solution(13182744141232754230)
XLA Ops:
  1.3 54.7 %shard_map.76 = (f32[5,16,256]{2,1,0:T(8,128)S(1)}, f32[4,4,16,16]{3,2,1,0:T(8,128)S(1)}, f32[5,16,16]{2,1,0:T(8,128)S(1)}) custom-call(f32[16,256]{1,0:T(8,128)} %start_ref.1, f32[32,256,256]{2,1,0:T(8,128)} %bitcast.5, s32[1,32]{1,0:T(1,128)} %bitcast.6, s32[1,32]{1,0:T(1,128)} %bitcast.7, s32[1]{0:T(128)} %bitcast.4.count_ref), custom_call_target="tpu_custom_call" | custom-call | tf_op jit(solution)/shard_map/pallas_call | solution.py:545
  56.0 0.7 %shard_map.77 = (f32[5,16,256]{2,1,0:T(8,128)}, f32[4,4,16,16]{3,2,1,0:T(8,128)}, f32[5,16,16]{2,1,0:T(8,128)}) custom-call(f32[5,16,256]{2,1,0:T(8,128)S(1)} %get-tuple-element.6.basis, f32[4,4,16,16]{3,2,1,0:T(8,128)S(1)} %get-tuple-element.7.proj, f32[5,16,16]{2,1,0:T(8,128)S(1)} %get-tuple-element.8.factors), custom_call_target="tpu_custom_call" | custom-call | tf_op jit(solution)/shard_map/pallas_call | solution.py:599

commit v4 on v3

--- a/solution.py
+++ b/solution.py
@@ -85,9 +85,9 @@
     start_ref, tiles_ref, row_ref, col_ref, count_ref,
     basis_ref, proj_ref, factors_ref,
     raw, merged, high, low, high_t, low_t, rows_v, cols_v, table_v, table,
-    u_ref, lr_ref, stack, lstack, row_panel, col_panel, row_split, col_split,
+    u_ref, v_ref, lr_ref, stack, lstack, row_panel, col_panel, row_split, col_split,
     acc_row, acc_col, got_row, got_col, deg_row, deg_col, deg_got_row, deg_got_col,
-    degree_ref, sigma_ref, coeff_ref, red_col, red_grp, early, late,
+    degree_ref, sigma_ref, shift_ref, left_ref, upper_ref, coeff_ref, red_col, red_grp, early, late,
     tile_sem, in_sem, gather_row_sem, gather_col_sem, scatter_row_sem, scatter_col_sem,
     deg_row_sem, deg_col_sem, red_col_sem, red_grp_sem, early_sem, late_sem,
 ):
@@ -133,14 +133,14 @@
     everyone = grp_size * col_size
     lax.fori_loop(1, everyone, greet, 0, unroll=everyone <= 32)
 
-    def copy_to(axis, d, source, target, sems):
+    def copy_to(axis, d, source, target, send_sem, recv_sem):
         size = col_size if axis == "col" else grp_size
         peer = flip(col if axis == "col" else grp, d, size)
         return pltpu.make_async_remote_copy(
             src_ref=source(peer),
             dst_ref=target,
-            send_sem=sems.at[0],
-            recv_sem=sems.at[1],
+            send_sem=send_sem,
+            recv_sem=recv_sem,
             device_id=(grp, peer) if axis == "col" else (peer, col),
             device_id_type=MESH,
         )
@@ -149,29 +149,45 @@
         size = col_size if axis == "col" else grp_size
 
         def visit(d, carry):
-            copy_to(axis, size - d, source, target, sems).start()
+            copy_to(axis, size - d, source, target, sems.at[0], sems.at[1]).start()
             return carry
 
         lax.fori_loop(1, size, visit, 0, unroll=size <= 8)
 
+    def bytes_of(part, send_sem, recv_sem):
+        return pltpu.make_async_remote_copy(
+            src_ref=part, dst_ref=part, send_sem=send_sem, recv_sem=recv_sem,
+            device_id=other(1), device_id_type=MESH,
+        )
+
     def await_all(buf, sems):
-        part = buf.at[pl.ds(0, buf.shape[0] - 1)]
-        pltpu.make_async_remote_copy(
-            src_ref=part, dst_ref=part, send_sem=sems.at[0], recv_sem=sems.at[1],
-            device_id=other(1), device_id_type=MESH,
-        ).wait()
-
-    def gather_col(par, start):
-        if start:
-            send("grp", lambda peer: u_ref.at[par], col_panel.at[par, grp], gather_col_sem.at[par])
-        else:
-            await_all(col_panel.at[par], gather_col_sem.at[par])
-
-    def gather_row(par, start):
-        if start:
-            send("col", lambda peer: u_ref.at[par], row_panel.at[par, col], gather_row_sem.at[par])
-        else:
-            await_all(row_panel.at[par], gather_row_sem.at[par])
+        bytes_of(buf.at[pl.ds(0, buf.shape[0] - 1)], sems.at[0], sems.at[1]).wait()
+
+    col_groups = ((1, grp_size - 1), (grp_size - 1, grp_size))
+    row_groups = ((1, 2), (2, 4), (4, col_size))
+
+    def gather(axis, par, panel, sems, groups):
+        me = col if axis == "col" else grp
+        for n, (low_d, high_d) in reversed(list(enumerate(groups))):
+
+            def visit(i, carry):
+                d = high_d - 1 - i
+                target = panel.at[par, me]
+                copy_to(axis, d, lambda peer: u_ref.at[par], target, sems.at[par, 0], sems.at[par, n + 1]).start()
+                return carry
+
+            lax.fori_loop(0, high_d - low_d, visit, 0, unroll=high_d - low_d <= 8)
+
+    def arrive(par, panel, sems, groups, n):
+        count = groups[n][1] - groups[n][0]
+        bytes_of(panel.at[par, pl.ds(0, count)], sems.at[par, 0], sems.at[par, n + 1]).wait_recv()
+
+    def leave(par, panel, sems):
+        count = panel.shape[1] - 1
+        bytes_of(panel.at[par, pl.ds(0, count)], sems.at[par, 0], sems.at[par, 1]).wait_send()
+
+    col_side = (col_panel, gather_col_sem, col_groups)
+    row_side = (row_panel, gather_row_sem, row_groups)
 
     def spread(axis, buf, sems, start):
         me = col if axis == "col" else grp
@@ -196,98 +212,117 @@
         return table[0, r * grp_size + q]
 
     def send_rows(par, r, d, with_degree):
-        copy_to("col", d, lambda peer: acc_row.at[r], got_row.at[par, col], scatter_row_sem.at[par]).start()
+        sems = scatter_row_sem.at[par]
+        copy_to("col", d, lambda peer: acc_row.at[r], got_row.at[par, col], sems.at[0], sems.at[1]).start()
         if with_degree:
-            copy_to("col", d, lambda peer: deg_row.at[r], deg_got_row.at[col], deg_row_sem).start()
-
-    def halves(panel, par, size, split, with_degree):
+            sems = deg_row_sem
+            copy_to("col", d, lambda peer: deg_row.at[r], deg_got_row.at[col], sems.at[0], sems.at[1]).start()
+
+    def halves(panel, par, size, split):
         for place in range(size):
             first, second = split_two(panel[par, place])
             at = pl.ds(place * tile_size, tile_size)
             split[:width, at] = first
-            if with_degree:
-                split[width : 2 * width, at] = jnp.ones((width, tile_size), BF16)
-                split[2 * width :, at] = second
-            else:
-                split[width : 2 * width, at] = second
-
-    def combine(total, rest, with_degree):
-        if not with_degree:
-            return total[:width] + total[width:] + rest, None
+            split[width : 2 * width, at] = jnp.ones((width, tile_size), BF16)
+            split[2 * width :, at] = second
+
+    def combine(total, rest):
         piece = total[:width] + total[2 * width :] + rest[:width]
         return piece, total[width : width + 1] + rest[width : width + 1]
 
-    def rows_of(r, with_degree):
+    def rows_of(r):
         places = [position(r, q) for q in range(grp_size)]
-        if with_degree:
-            left = col_split[...]
-            firsts = jnp.concatenate([high[p] for p in places], axis=1)
-            seconds = jnp.concatenate([low[p] for p in places], axis=1)
-            return combine(dot_nt(left, firsts), dot_nt(left[: 2 * width], seconds), True)
-        left = col_split[: 2 * width]
-        firsts = jnp.concatenate([high_t[p] for p in places], axis=0)
-        seconds = jnp.concatenate([low_t[p] for p in places], axis=0)
-        return combine(dot_nn(left, firsts), dot_nn(left[:width], seconds), False)
-
-    def cols_of(q, with_degree):
+        left = col_split[...]
+        firsts = jnp.concatenate([high[p] for p in places], axis=1)
+        seconds = jnp.concatenate([low[p] for p in places], axis=1)
+        return combine(dot_nt(left, firsts), dot_nt(left[: 2 * width], seconds))
+
+    def cols_of(q):
         piece, degree = 0.0, 0.0
-        chunk = CHUNK if col_size % CHUNK == 0 else 1
-        for base in range(0, col_size, chunk):
-            at = pl.ds(base * tile_size, chunk * tile_size)
-            left = row_split[:, at] if with_degree else row_split[: 2 * width, at]
-            places = [position(base + r, q) for r in range(chunk)]
+        for base in range(0, col_size, CHUNK):
+            left = row_split[:, pl.ds(base * tile_size, CHUNK * tile_size)]
+            places = [position(base + r, q) for r in range(CHUNK)]
             firsts = jnp.concatenate([high[p] for p in places], axis=0)
             seconds = jnp.concatenate([low[p] for p in places], axis=0)
-            rest = dot_nn(left[: 2 * width] if with_degree else left[:width], seconds)
-            part, extra = combine(dot_nn(left, firsts), rest, with_degree)
+            part, extra = combine(dot_nn(left, firsts), dot_nn(left[: 2 * width], seconds))
             piece = piece + part
-            if with_degree:
-                degree = degree + extra
+            degree = degree + extra
         return piece, degree
 
-    def all_rows(par, with_degree):
-        def visit(d, carry):
+    def first_rows():
+        def visit(d):
             r = flip(col, d, col_size)
-            piece, degree = rows_of(r, with_degree)
+            piece, degree = rows_of(r)
             acc_row[r] = piece
-            if with_degree:
-                deg_row[r] = degree
-            return carry
+            deg_row[r] = degree
+
+        def go(base, count):
+            for i in range(count):
+                visit(base + i)
+            for i in range(count):
+                send_rows(0, flip(col, base + i, col_size), base + i, True)
 
         if col_size <= 8:
-            order = list(range(col_size - 1, -1, -1))
-            for base in range(0, col_size, 4):
-                for d in order[base : base + 4]:
-                    visit(d, 0)
-                for d in order[base : base + 4]:
-                    if d:
-                        send_rows(par, flip(col, d, col_size), d, with_degree)
+            go(col_size // 2, col_size // 2)
+            go(1, col_size // 2 - 1)
         else:
-            def go(d, carry):
-                visit(d, 0)
-                send_rows(par, flip(col, d, col_size), d, with_degree)
+            def each(d, carry):
+                go(d, 1)
                 return carry
 
-            lax.fori_loop(1, col_size, go, 0)
-            visit(0, 0)
-        got_row[par, col] = acc_row[col]
-        if with_degree:
-            deg_got_row[col] = deg_row[col]
-
-    def all_cols(par, with_degree):
+            lax.fori_loop(1, col_size, each, 0)
+        visit(0)
+        got_row[0, col] = acc_row[col]
+        deg_got_row[col] = deg_row[col]
+
+    def first_cols():
         for d in range(grp_size - 1, -1, -1):
             q = flip(grp, d, grp_size)
-            piece, degree = cols_of(q, with_degree)
+            piece, degree = cols_of(q)
             acc_col[q] = piece
-            if with_degree:
-                deg_col[q] = degree
-        send("grp", lambda peer: acc_col.at[peer], got_col.at[par, grp], scatter_col_sem.at[par])
-        got_col[par, grp] = acc_col[grp]
-        if with_degree:
-            send("grp", lambda peer: deg_col.at[peer], deg_got_col.at[grp], deg_col_sem)
-            deg_got_col[grp] = deg_col[grp]
+            deg_col[q] = degree
+        send("grp", lambda peer: acc_col.at[peer], got_col.at[0, grp], scatter_col_sem.at[0])
+        got_col[0, grp] = acc_col[grp]
+        send("grp", lambda peer: deg_col.at[peer], deg_got_col.at[grp], deg_col_sem)
+        deg_got_col[grp] = deg_col[grp]
+
+    def stacked(pieces):
+        pairs = [split_two(piece) for piece in pieces]
+        return jnp.concatenate([jnp.concatenate(pair, axis=0) for pair in pairs], axis=1)
+
+    def product(left, firsts, seconds):
+        total = dot_nn(left, jnp.concatenate(firsts, axis=0))
+        rest = dot_nn(left[:width], jnp.concatenate(seconds, axis=0))
+        return total[:width] + total[width:] + rest
+
+    def rows_batch(par, ds):
+        places = [flip(grp, d, grp_size) for d in ds]
+        left = stacked([u_ref[par] if d == 0 else col_panel[par, q] for d, q in zip(ds, places)])
+
+        def visit(r, carry):
+            at = [position(r, q) for q in places]
+            piece = product(left, [high_t[p] for p in at], [low_t[p] for p in at])
+            acc_row[r] = piece if ds[0] == 0 else acc_row[r] + piece
+            return carry
+
+        if col_size <= 8:
+            for r in range(col_size):
+                visit(r, 0)
+        else:
+            lax.fori_loop(0, col_size, visit, 0)
+
+    def cols_batch(par, base, count):
+        places = [flip(col, base + i, col_size) for i in range(count)]
+        own = isinstance(base, int) and base == 0
+        left = stacked([u_ref[par]] if own else [row_panel[par, r] for r in places])
+        for q in range(grp_size):
+            at = [position(r, q) for r in places]
+            piece = product(left, [high[p] for p in at], [low[p] for p in at])
+            acc_col[q] = piece if own else acc_col[q] + piece
 
     def collect(par, with_degree):
+        leave(par, col_panel, gather_col_sem)
+        leave(par, row_panel, gather_row_sem)
         await_all(got_row.at[par], scatter_row_sem.at[par])
         await_all(got_col.at[par], scatter_col_sem.at[par])
         if with_degree:
@@ -297,18 +332,8 @@
         total = jnp.sum(got_row[par], axis=0) + jnp.sum(got_col[par], axis=0)
         return degree_ref[...] * u_ref[par] - total
 
-    loads[0].wait()
     stack[...] = jnp.zeros_like(stack)
     lstack[...] = jnp.zeros_like(lstack)
-    start = u_ref[0]
-    stack[0] = start
-    stack[1] = start
-    row_panel[0, col] = start
-    col_panel[0, grp] = start
-    pl.semaphore_wait(barrier, everyone - 1)
-    gather_col(0, True)
-    gather_row(0, True)
-
     loads[1].wait()
     loads[2].wait()
     spots = table.shape[1]
@@ -338,27 +363,41 @@
     low[slots] = empty.astype(BF16)
     high_t[slots] = empty.astype(BF16)
     low_t[slots] = empty.astype(BF16)
+    loads[0].wait()
+    start = u_ref[0]
+    stack[0] = start
+    stack[1] = start
+    row_panel[0, col] = start
+    col_panel[0, grp] = start
+    pl.semaphore_wait(barrier, everyone - 1)
+    gather("grp", 0, *col_side)
+    gather("col", 0, *row_side)
     move.wait()
 
     def merge(n, carry):
         load_tile(n).wait()
-        for m in range(share):
+
+        def visit(m, carry):
             s = n * share + m
             value = raw[s] + merged[table[1, s]]
             merged[s] = value
             first, second = split_two(value)
             high[s] = first
             low[s] = second
-        return carry
+            return carry
+
+        return lax.fori_loop(0, share, visit, carry)
 
     lax.fori_loop(0, loads_of, merge, 0)
 
-    gather_col(0, False)
-    halves(col_panel, 0, grp_size, col_split, True)
-    all_rows(0, True)
-    gather_row(0, False)
-    halves(row_panel, 0, col_size, row_split, True)
-    all_cols(0, True)
+    for n in range(len(col_groups)):
+        arrive(0, *col_side, n)
+    halves(col_panel, 0, grp_size, col_split)
+    first_rows()
+    for n in range(len(row_groups)):
+        arrive(0, *row_side, n)
+    halves(row_panel, 0, col_size, row_split)
+    first_cols()
 
     def turn(s, carry):
         high_t[s] = high[s].T
@@ -368,8 +407,10 @@
     lax.fori_loop(0, slots, turn, 0, unroll=4)
     applied = collect(0, True)
     lr_ref[...] = applied
+    v_ref[...] = applied
     u_ref[1] = applied
     sigma_ref[...] = jnp.zeros_like(sigma_ref)
+    left_ref[ITERS] = jnp.where(lane == row, 1.0, 0.0)
 
     half = width // 2
 
@@ -383,63 +424,73 @@
             [jnp.where(low_lanes, packed, turned), jnp.where(low_lanes, turned, packed)], axis=0
         )
 
-    def settle(total, inverse):
+    def step(k, carry):
+        par = lax.rem(k + 1, 2)
+        block_u, block_r = u_ref[par], stack[1]
+        gather("grp", par, *col_side)
+        block = stack[0:4].reshape(4 * width, tile_size)
+        block = jnp.concatenate([block, block], axis=0)
+        both = dot_nt(jnp.concatenate([v_ref[...], block_r], axis=0), block, HIGHEST)
+        inner = lax.rem(lane, 4 * width)
+        red_grp[par, grp] = fold(jnp.where((inner >= width) & (inner < 2 * width), both[width:], both[:width]))
+        spread("grp", red_grp.at[par], red_grp_sem.at[par], True)
+        gather("col", par, *row_side)
+
+        rows_batch(par, [0])
+        cols_batch(par, 0, 1)
+        arrive(par, *row_side, 0)
+        cols_batch(par, 1, 1)
+        arrive(par, *col_side, 0)
+        rows_batch(par, list(range(1, grp_size - 1)))
+        spread("grp", red_grp.at[par], red_grp_sem.at[par], False)
+        red_col[par, col] = jnp.sum(red_grp[par], axis=0)
+        spread("col", red_col.at[par], red_col_sem.at[par], True)
+        arrive(par, *col_side, 1)
+        rows_batch(par, [grp_size - 1])
+        send("col", lambda peer: acc_row.at[peer], got_row.at[par, col], scatter_row_sem.at[par])
+        got_row[par, col] = acc_row[col]
+        arrive(par, *row_side, 1)
+        cols_batch(par, 2, 2)
+        arrive(par, *row_side, 2)
+        if col_size <= 8:
+            cols_batch(par, 4, col_size - 4)
+        else:
+            def visit(n, carry):
+                cols_batch(par, 4 * n, 4)
+                return carry
+
+            lax.fori_loop(1, col_size // 4, visit, 0)
+        send("grp", lambda peer: acc_col.at[peer], got_col.at[par, grp], scatter_col_sem.at[par])
+        got_col[par, grp] = acc_col[grp]
+
+        spread("col", red_col.at[par], red_col_sem.at[par], False)
+        total = unfold(jnp.sum(red_col[par], axis=0) / node_total)
+        former = left_ref[lax.rem(k + ITERS, ITERS + 1)]
+        turned = dot_nn(former[:, :width], total, HIGHEST)
+        upper, inverse = factorize(total)
         left = inverse[:, :width]
-        fresh = dot_nn(left, jnp.concatenate([stack[1], lr_ref[...]], axis=1), HIGHEST)
+        fresh = dot_nn(left, jnp.concatenate([block_r, lr_ref[...]], axis=1), HIGHEST)
         newest, image = fresh[:, :tile_size], fresh[:, tile_size:]
         pad = jnp.concatenate([inverse, jnp.zeros((LANES - width, LANES), F32)], axis=0)
-        mixed = dot_nt(total[:, :width], pad[:, :width], HIGHEST)
-        coeffs = jnp.where(lane < width, mixed, jnp.where((lane >= 2 * width) & (lane < 5 * width), total, 0.0))
+        mixed = dot_nt(turned[:, :width], pad[:, :width], HIGHEST)
+        older = (lane >= 2 * width) & (lane < 4 * width)
+        coeffs = jnp.where(lane < width, mixed, jnp.where(older, turned, 0.0))
         stack[0] = newest
         lstack[0] = image
-        return left, newest, image, coeffs
-
-    def step(k, carry):
-        par = lax.rem(k + 1, 2)
-        row_panel[par, col] = u_ref[par]
-        col_panel[par, grp] = u_ref[par]
-        gather_col(par, True)
-        gather_row(par, True)
-        block = stack[0:4].reshape(4 * width, tile_size)
-        block = jnp.concatenate([block, block], axis=0)
-        both = dot_nt(jnp.concatenate([u_ref[par], stack[1]], axis=0), block, HIGHEST)
-        gram_lanes = (lax.rem(lane, 4 * width) >= width) & (lax.rem(lane, 4 * width) < 2 * width)
-        part = jnp.where(gram_lanes, both[width:], both[:width])
-        red_col[par, col] = fold(part)
-        spread("col", red_col.at[par], red_col_sem.at[par], True)
-
-        gather_col(par, False)
-        halves(col_panel, par, grp_size, col_split, False)
-        all_rows(par, False)
-
-        spread("col", red_col.at[par], red_col_sem.at[par], False)
-        red_grp[par, grp] = jnp.sum(red_col[par], axis=0)
-        spread("grp", red_grp.at[par], red_grp_sem.at[par], True)
-
-        gather_row(par, False)
-        halves(row_panel, par, col_size, row_split, False)
-        all_cols(par, False)
-
-        spread("grp", red_grp.at[par], red_grp_sem.at[par], False)
-        total = jnp.where(lane < LANES // 2, unfold(jnp.sum(red_grp[par], axis=0) / node_total), 0.0)
-        upper, inverse = factorize(total)
-        left, newest, image, coeffs = settle(total, inverse)
-        factors_ref[k] = factor_of(upper)
-        basis_ref[k] = newest
         now = dot_nn(coeffs, jnp.concatenate([stack[...].reshape(LANES, tile_size),
                                               lstack[...].reshape(LANES, tile_size)], axis=1), HIGHEST)
-        residual = dot_nn(left, u_ref[par] - now[:, :tile_size], HIGHEST)
-        known = now[:, tile_size:]
-        found = dot_nn(left, coeffs, HIGHEST)
-        found = found + jnp.where(lane == row, sigma_ref[:, :LANES], 0.0)
-        coeff_ref[k] = found
-        mean = jnp.sum(jnp.where(lane == row, found, 0.0), axis=1, keepdims=True)
-        mean = jnp.sum(mean, axis=0, keepdims=True) / width
-        sigma = jnp.where(k == 0, jnp.broadcast_to(mean, sigma_ref.shape), sigma_ref[...])
+        rest = block_u - now[:, :tile_size]
+        residual = dot_nn(left, rest, HIGHEST)
+        on_block = jnp.sum(jnp.where(lane == row, total, 0.0), axis=1, keepdims=True)
+        on_gram = jnp.sum(jnp.where(lane == row + width, total, 0.0), axis=1, keepdims=True)
+        mean = jnp.sum(on_block, axis=0, keepdims=True) / jnp.sum(on_gram, axis=0, keepdims=True)
+        before = sigma_ref[...]
+        sigma = jnp.where(k == 0, jnp.broadcast_to(mean, sigma_ref.shape), before)
+        known = now[:, tile_size:] + sigma * rest
+        stack[0] = residual
+        stack[1] = residual
         stack[k + 2] = newest
         lstack[k + 2] = image
-        stack[0] = residual
-        stack[1] = residual
 
         @pl.when(k == ITERS - 2)
         def _():
@@ -448,11 +499,18 @@
             early[grp * col_size + col] = fold(dot_nt(residual, block, HIGHEST))
             spread_all(early, early_sem)
 
-        applied = collect(par, False)
-        image_next = dot_nn(left, applied - known, HIGHEST)
-        lr_ref[...] = image_next
-        u_ref[1 - par] = image_next - sigma * residual
+        basis_ref[k] = newest
+        left_ref[k] = inverse
+        upper_ref[k] = upper
+        coeff_ref[k] = coeffs
         sigma_ref[...] = sigma
+        shift_ref[k] = before[:, :LANES]
+
+        applied = collect(par, False) - known
+        fresh_u = dot_nn(left, applied, HIGHEST)
+        v_ref[...] = applied
+        u_ref[1 - par] = fresh_u
+        lr_ref[...] = fresh_u + sigma * residual
         return carry
 
     lax.fori_loop(0, ITERS - 1, step, 0)
@@ -478,13 +536,15 @@
     pad = jnp.concatenate([inverse, jnp.zeros((LANES - width, LANES), F32)], axis=0)[:, :width]
     proj_ref[...] = jnp.zeros_like(proj_ref)
 
-    def keep_coeffs(k):
+    def keep_coeffs(k, left, coeffs, shift):
+        found = dot_nn(left, coeffs, HIGHEST) + jnp.where(lane == row, shift, 0.0)
         for j in range(k):
-            proj_ref[k, j] = coeff_ref[k, :, (j + 2) * width : (j + 3) * width]
-        proj_ref[k, k] = coeff_ref[k, :, :width]
+            proj_ref[k, j] = found[:, (j + 2) * width : (j + 3) * width]
+        proj_ref[k, k] = found[:, :width]
 
     for n in range(ITERS - 1):
-        keep_coeffs(n)
+        keep_coeffs(n, left_ref[n, :, :width], coeff_ref[n], shift_ref[n])
+        factors_ref[n] = factor_of(upper_ref[n])
     await_all(late, late_sem)
     packed = jnp.sum(late[...], axis=0) / node_total
     total = jnp.concatenate(
@@ -498,8 +558,7 @@
     upper, inverse = factorize(gram)
     basis_ref[ITERS] = dot_nn(inverse[:, :width], rest, HIGHEST)
     factors_ref[ITERS] = dot_nt(left, upper[:, width : 2 * width], HIGHEST)
-    coeff_ref[k] = dot_nn(left, coeffs, HIGHEST) + jnp.where(lane == row, sigma_ref[:, :LANES], 0.0)
-    keep_coeffs(k)
+    keep_coeffs(k, left, coeffs, sigma_ref[:, :LANES])
 
 
 def deliver(basis, proj, factors, basis_out, proj_out, factors_out, sem):
@@ -518,6 +577,7 @@
         width, shard_len = start_block.shape
         slots, tile_size = tile_values.shape[2], tile_values.shape[3]
         assert shard_len == tile_size and LANES // width == 8
+        assert grp_size > 2 and col_size % CHUNK == 0
         assert grp_size & (grp_size - 1) == 0 and col_size & (col_size - 1) == 0
         places = LANES // width
         node_total = shard_len * grp_size * col_size
@@ -560,6 +620,7 @@
                 pltpu.SMEM((8, spots), I32),
                 pltpu.VMEM((2,) + block, F32),
                 pltpu.VMEM(block, F32),
+                pltpu.VMEM(block, F32),
                 pltpu.VMEM((places,) + block, F32),
                 pltpu.VMEM((places,) + block, F32),
                 pltpu.VMEM((2, col_size) + block, F32),
@@ -577,13 +638,16 @@
                 pltpu.VMEM(line, F32),
                 pltpu.VMEM(block, F32),
                 pltpu.VMEM((ITERS,) + small, F32),
+                pltpu.VMEM((ITERS + 1,) + small, F32),
+                pltpu.VMEM((ITERS,) + small, F32),
+                pltpu.VMEM((ITERS,) + small, F32),
                 pltpu.VMEM((2, col_size) + packed, F32),
                 pltpu.VMEM((2, grp_size) + packed, F32),
                 pltpu.VMEM((grp_size * col_size,) + packed, F32),
                 pltpu.VMEM((grp_size * col_size, width // 4, LANES), F32),
                 sems(8 if slots % 8 == 0 else slots),
                 sems(4),
-                sems(2, 2), sems(2, 2), sems(2, 2), sems(2, 2),
+                sems(2, 4), sems(2, 3), sems(2, 2), sems(2, 2),
                 sems(2), sems(2), sems(2, 2), sems(2, 2), sems(2), sems(2),
             ],
             compiler_params=pltpu.CompilerParams(

time: 57 us -> 55.9 us (0.981)
  Pallas kernels: 55.4 us -> 54.4 us
    pallas_call x1, Pallas kernels: 54.7 us -> 53.6 us  [body(): pl.pallas_call(functools.partial(kernel, grp_size, col_size, node_total),...]
where the time goes in v4:
time: 55.9 us; the launch traced here: 55.6 us
  Pallas kernels  54.4 us (97%)
  between operations  1.29 us (2%)
    pallas_call x1, Pallas kernels, body(): pl.pallas_call(functools.partial(kernel, grp_size, col_size, node_total),...  53.6 us

profile of v4, /device:TPU:0, one launch (start us, length us, event | category | flops | bytes accessed | tf_op | source)
XLA Modules:
  0.0 55.6 jit_solution(1681064520257404782)
XLA Ops:
  1.3 53.6 %shard_map.76 = (f32[5,16,256]{2,1,0:T(8,128)S(1)}, f32[4,4,16,16]{3,2,1,0:T(8,128)S(1)}, f32[5,16,16]{2,1,0:T(8,128)S(1)}) custom-call(f32[16,256]{1,0:T(8,128)} %start_ref.1, f32[32,256,256]{2,1,0:T(8,128)} %bitcast.5, s32[1,32]{1,0:T(1,128)} %bitcast.6, s32[1,32]{1,0:T(1,128)} %bitcast.7, s32[1]{0:T(128)} %bitcast.4.count_ref), custom_call_target="tpu_custom_call" | custom-call | tf_op jit(solution)/shard_map/pallas_call | solution.py:605
  54.9 0.7 %shard_map.77 = (f32[5,16,256]{2,1,0:T(8,128)}, f32[4,4,16,16]{3,2,1,0:T(8,128)}, f32[5,16,16]{2,1,0:T(8,128)}) custom-call(f32[5,16,256]{2,1,0:T(8,128)S(1)} %get-tuple-element.6.basis, f32[4,4,16,16]{3,2,1,0:T(8,128)S(1)} %get-tuple-element.7.proj, f32[5,16,16]{2,1,0:T(8,128)S(1)} %get-tuple-element.8.factors), custom_call_target="tpu_custom_call" | custom-call | tf_op jit(solution)/shard_map/pallas_call | solution.py:663

commit v5 on v4

--- a/solution.py
+++ b/solution.py
@@ -15,7 +15,7 @@
 I32 = jnp.int32
 LANES = 128
 CHUNK = 8
-STRIDE = 4
+STRIDE = 8
 
 
 def dot_nt(left, right, precision=None):
@@ -85,7 +85,7 @@
     start_ref, tiles_ref, row_ref, col_ref, count_ref,
     basis_ref, proj_ref, factors_ref,
     raw, merged, high, low, high_t, low_t, rows_v, cols_v, table_v, table,
-    u_ref, v_ref, lr_ref, stack, lstack, row_panel, col_panel, row_split, col_split,
+    u_ref, lr_ref, stack, lstack, row_panel, col_panel, row_split, col_split,
     acc_row, acc_col, got_row, got_col, deg_row, deg_col, deg_got_row, deg_got_col,
     degree_ref, sigma_ref, shift_ref, left_ref, upper_ref, coeff_ref, red_col, red_grp, early, late,
     tile_sem, in_sem, gather_row_sem, gather_col_sem, scatter_row_sem, scatter_col_sem,
@@ -256,22 +256,23 @@
             acc_row[r] = piece
             deg_row[r] = degree
 
-        def go(base, count):
-            for i in range(count):
-                visit(base + i)
-            for i in range(count):
-                send_rows(0, flip(col, base + i, col_size), base + i, True)
+        def go(ds):
+            for d in ds:
+                visit(d)
+            for d in ds:
+                if not isinstance(d, int) or d:
+                    send_rows(0, flip(col, d, col_size), d, True)
 
         if col_size <= 8:
-            go(col_size // 2, col_size // 2)
-            go(1, col_size // 2 - 1)
+            go(range(col_size // 2, col_size))
+            go(range(col_size // 2))
         else:
             def each(d, carry):
-                go(d, 1)
+                go([d])
                 return carry
 
             lax.fori_loop(1, col_size, each, 0)
-        visit(0)
+            visit(0)
         got_row[0, col] = acc_row[col]
         deg_got_row[col] = deg_row[col]
 
@@ -407,7 +408,6 @@
     lax.fori_loop(0, slots, turn, 0, unroll=4)
     applied = collect(0, True)
     lr_ref[...] = applied
-    v_ref[...] = applied
     u_ref[1] = applied
     sigma_ref[...] = jnp.zeros_like(sigma_ref)
     left_ref[ITERS] = jnp.where(lane == row, 1.0, 0.0)
@@ -424,33 +424,36 @@
             [jnp.where(low_lanes, packed, turned), jnp.where(low_lanes, turned, packed)], axis=0
         )
 
+    def inner_products(par, block_v):
+        block = stack[0:4].reshape(4 * width, tile_size)
+        block = jnp.concatenate([block, block], axis=0)
+        both = dot_nt(jnp.concatenate([block_v, stack[1]], axis=0), block, HIGHEST)
+        inner = lax.rem(lane, 4 * width)
+        red_grp[par, grp] = fold(jnp.where((inner >= width) & (inner < 2 * width), both[width:], both[:width]))
+
+    inner_products(1, applied)
+
     def step(k, carry):
         par = lax.rem(k + 1, 2)
         block_u, block_r = u_ref[par], stack[1]
         gather("grp", par, *col_side)
-        block = stack[0:4].reshape(4 * width, tile_size)
-        block = jnp.concatenate([block, block], axis=0)
-        both = dot_nt(jnp.concatenate([v_ref[...], block_r], axis=0), block, HIGHEST)
-        inner = lax.rem(lane, 4 * width)
-        red_grp[par, grp] = fold(jnp.where((inner >= width) & (inner < 2 * width), both[width:], both[:width]))
         spread("grp", red_grp.at[par], red_grp_sem.at[par], True)
         gather("col", par, *row_side)
 
         rows_batch(par, [0])
         cols_batch(par, 0, 1)
-        arrive(par, *row_side, 0)
-        cols_batch(par, 1, 1)
         arrive(par, *col_side, 0)
-        rows_batch(par, list(range(1, grp_size - 1)))
         spread("grp", red_grp.at[par], red_grp_sem.at[par], False)
         red_col[par, col] = jnp.sum(red_grp[par], axis=0)
         spread("col", red_col.at[par], red_col_sem.at[par], True)
         arrive(par, *col_side, 1)
+        rows_batch(par, list(range(1, grp_size - 1)))
         rows_batch(par, [grp_size - 1])
         send("col", lambda peer: acc_row.at[peer], got_row.at[par, col], scatter_row_sem.at[par])
         got_row[par, col] = acc_row[col]
+        arrive(par, *row_side, 0)
         arrive(par, *row_side, 1)
-        cols_batch(par, 2, 2)
+        cols_batch(par, 1, 3)
         arrive(par, *row_side, 2)
         if col_size <= 8:
             cols_batch(par, 4, col_size - 4)
@@ -481,11 +484,11 @@
                                               lstack[...].reshape(LANES, tile_size)], axis=1), HIGHEST)
         rest = block_u - now[:, :tile_size]
         residual = dot_nn(left, rest, HIGHEST)
-        on_block = jnp.sum(jnp.where(lane == row, total, 0.0), axis=1, keepdims=True)
+        on_block = jnp.sum(jnp.where(lane == row, turned, 0.0), axis=1, keepdims=True)
         on_gram = jnp.sum(jnp.where(lane == row + width, total, 0.0), axis=1, keepdims=True)
         mean = jnp.sum(on_block, axis=0, keepdims=True) / jnp.sum(on_gram, axis=0, keepdims=True)
         before = sigma_ref[...]
-        sigma = jnp.where(k == 0, jnp.broadcast_to(mean, sigma_ref.shape), before)
+        sigma = before + jnp.broadcast_to(mean, sigma_ref.shape)
         known = now[:, tile_size:] + sigma * rest
         stack[0] = residual
         stack[1] = residual
@@ -508,7 +511,7 @@
 
         applied = collect(par, False) - known
         fresh_u = dot_nn(left, applied, HIGHEST)
-        v_ref[...] = applied
+        inner_products(1 - par, applied)
         u_ref[1 - par] = fresh_u
         lr_ref[...] = fresh_u + sigma * residual
         return carry
@@ -619,7 +622,6 @@
                 pltpu.VMEM((8, spots), I32),
                 pltpu.SMEM((8, spots), I32),
                 pltpu.VMEM((2,) + block, F32),
-                pltpu.VMEM(block, F32),
                 pltpu.VMEM(block, F32),
                 pltpu.VMEM((places,) + block, F32),
                 pltpu.VMEM((places,) + block, F32),

time: 55.9 us -> 55.4 us (level)
  no operation moved by 1% of the time
where the time goes in v5:
time: 55.4 us; the launch traced here: 55.2 us
  Pallas kernels  53.9 us (97%)
  between operations  1.29 us (2%)
    pallas_call x1, Pallas kernels, body(): pl.pallas_call(functools.partial(kernel, grp_size, col_size, node_total),...  53.2 us

profile of v5, /device:TPU:0, one launch (start us, length us, event | category | flops | bytes accessed | tf_op | source)
XLA Modules:
  0.0 55.2 jit_solution(6255141847623908244)
XLA Ops:
  1.3 53.2 %shard_map.76 = (f32[5,16,256]{2,1,0:T(8,128)S(1)}, f32[4,4,16,16]{3,2,1,0:T(8,128)S(1)}, f32[5,16,16]{2,1,0:T(8,128)S(1)}) custom-call(f32[16,256]{1,0:T(8,128)} %start_ref.1, f32[32,256,256]{2,1,0:T(8,128)} %bitcast.5, s32[1,32]{1,0:T(1,128)} %bitcast.6, s32[1,32]{1,0:T(1,128)} %bitcast.7, s32[1]{0:T(128)} %bitcast.4.count_ref), custom_call_target="tpu_custom_call" | custom-call | tf_op jit(solution)/shard_map/pallas_call | solution.py:608
  54.5 0.7 %shard_map.77 = (f32[5,16,256]{2,1,0:T(8,128)}, f32[4,4,16,16]{3,2,1,0:T(8,128)}, f32[5,16,16]{2,1,0:T(8,128)}) custom-call(f32[5,16,256]{2,1,0:T(8,128)S(1)} %get-tuple-element.6.basis, f32[4,4,16,16]{3,2,1,0:T(8,128)S(1)} %get-tuple-element.7.proj, f32[5,16,16]{2,1,0:T(8,128)S(1)} %get-tuple-element.8.factors), custom_call_target="tpu_custom_call" | custom-call | tf_op jit(solution)/shard_map/pallas_call | solution.py:665

commit v6 on v5

--- a/solution.py
+++ b/solution.py
@@ -16,6 +16,7 @@
 LANES = 128
 CHUNK = 8
 STRIDE = 8
+UNROLL = 4
 
 
 def dot_nt(left, right, precision=None):
@@ -87,9 +88,9 @@
     raw, merged, high, low, high_t, low_t, rows_v, cols_v, table_v, table,
     u_ref, lr_ref, stack, lstack, row_panel, col_panel, row_split, col_split,
     acc_row, acc_col, got_row, got_col, deg_row, deg_col, deg_got_row, deg_got_col,
-    degree_ref, sigma_ref, shift_ref, left_ref, upper_ref, coeff_ref, red_col, red_grp, early, late,
+    degree_ref, sigma_ref, shift_ref, left_ref, upper_ref, coeff_ref, red_col, red_grp, early_grp, early_col, late,
     tile_sem, in_sem, gather_row_sem, gather_col_sem, scatter_row_sem, scatter_col_sem,
-    deg_row_sem, deg_col_sem, red_col_sem, red_grp_sem, early_sem, late_sem,
+    deg_row_sem, deg_col_sem, red_col_sem, red_grp_sem, early_grp_sem, early_col_sem, late_sem,
 ):
     grp = lax.axis_index("grp")
     col = lax.axis_index("col")
@@ -233,9 +234,9 @@
     def rows_of(r):
         places = [position(r, q) for q in range(grp_size)]
         left = col_split[...]
-        firsts = jnp.concatenate([high[p] for p in places], axis=1)
+        firsts = jnp.concatenate([high_t[p] for p in places], axis=0)
         seconds = jnp.concatenate([low[p] for p in places], axis=1)
-        return combine(dot_nt(left, firsts), dot_nt(left[: 2 * width], seconds))
+        return combine(dot_nn(left, firsts), dot_nt(left[: 2 * width], seconds))
 
     def cols_of(q):
         piece, degree = 0.0, 0.0
@@ -384,10 +385,11 @@
             merged[s] = value
             first, second = split_two(value)
             high[s] = first
+            high_t[s] = first.T
             low[s] = second
             return carry
 
-        return lax.fori_loop(0, share, visit, carry)
+        return lax.fori_loop(0, share, visit, carry, unroll=UNROLL)
 
     lax.fori_loop(0, loads_of, merge, 0)
 
@@ -401,7 +403,6 @@
     first_cols()
 
     def turn(s, carry):
-        high_t[s] = high[s].T
         low_t[s] = low[s].T
         return carry
 
@@ -431,23 +432,23 @@
         inner = lax.rem(lane, 4 * width)
         red_grp[par, grp] = fold(jnp.where((inner >= width) & (inner < 2 * width), both[width:], both[:width]))
 
+    gather("grp", 1, *col_side)
     inner_products(1, applied)
 
     def step(k, carry):
         par = lax.rem(k + 1, 2)
         block_u, block_r = u_ref[par], stack[1]
-        gather("grp", par, *col_side)
         spread("grp", red_grp.at[par], red_grp_sem.at[par], True)
         gather("col", par, *row_side)
 
         rows_batch(par, [0])
         cols_batch(par, 0, 1)
         arrive(par, *col_side, 0)
+        rows_batch(par, list(range(1, grp_size - 1)))
         spread("grp", red_grp.at[par], red_grp_sem.at[par], False)
         red_col[par, col] = jnp.sum(red_grp[par], axis=0)
         spread("col", red_col.at[par], red_col_sem.at[par], True)
         arrive(par, *col_side, 1)
-        rows_batch(par, list(range(1, grp_size - 1)))
         rows_batch(par, [grp_size - 1])
         send("col", lambda peer: acc_row.at[peer], got_row.at[par, col], scatter_row_sem.at[par])
         got_row[par, col] = acc_row[col]
@@ -499,8 +500,8 @@
         def _():
             shifted = [lstack[j] - sigma * stack[j] for j in (4, 2, 3)]
             block = jnp.concatenate([shifted[0], residual, shifted[1], shifted[2]] * 2, axis=0)
-            early[grp * col_size + col] = fold(dot_nt(residual, block, HIGHEST))
-            spread_all(early, early_sem)
+            early_grp[grp] = fold(dot_nt(residual, block, HIGHEST))
+            spread("grp", early_grp, early_grp_sem, True)
 
         basis_ref[k] = newest
         left_ref[k] = inverse
@@ -511,8 +512,13 @@
 
         applied = collect(par, False) - known
         fresh_u = dot_nn(left, applied, HIGHEST)
+        u_ref[1 - par] = fresh_u
+
+        @pl.when(k < ITERS - 2)
+        def _():
+            gather("grp", 1 - par, *col_side)
+
         inner_products(1 - par, applied)
-        u_ref[1 - par] = fresh_u
         lr_ref[...] = fresh_u + sigma * residual
         return carry
 
@@ -527,8 +533,22 @@
     odd = lax.rem(lax.div(lane[:quarter], 2 * width), 2) == 1
     late[grp * col_size + col] = jnp.where(odd, both[quarter:], both[:quarter])
     spread_all(late, late_sem)
-    await_all(early, early_sem)
-    total = unfold(jnp.sum(early[...], axis=0) / node_total)
+    spread("grp", early_grp, early_grp_sem, False)
+    early_col[col] = jnp.sum(early_grp[...], axis=0)
+    spread("col", early_col, early_col_sem, True)
+    proj_ref[...] = jnp.zeros_like(proj_ref)
+
+    def keep_coeffs(k, left, coeffs, shift):
+        found = dot_nn(left, coeffs, HIGHEST) + jnp.where(lane == row, shift, 0.0)
+        for j in range(k):
+            proj_ref[k, j] = found[:, (j + 2) * width : (j + 3) * width]
+        proj_ref[k, k] = found[:, :width]
+
+    for n in range(ITERS - 1):
+        keep_coeffs(n, left_ref[n, :, :width], coeff_ref[n], shift_ref[n])
+        factors_ref[n] = factor_of(upper_ref[n])
+    spread("col", early_col, early_col_sem, False)
+    total = unfold(jnp.sum(early_col[...], axis=0) / node_total)
     upper, inverse = factorize(total)
     left = inverse[:, :width]
     newest = dot_nn(left, block_r, HIGHEST)
@@ -537,17 +557,6 @@
     factors_ref[k] = factor_of(upper)
     older = jnp.where((lane >= 2 * width) & (lane < 5 * width), total, 0.0)
     pad = jnp.concatenate([inverse, jnp.zeros((LANES - width, LANES), F32)], axis=0)[:, :width]
-    proj_ref[...] = jnp.zeros_like(proj_ref)
-
-    def keep_coeffs(k, left, coeffs, shift):
-        found = dot_nn(left, coeffs, HIGHEST) + jnp.where(lane == row, shift, 0.0)
-        for j in range(k):
-            proj_ref[k, j] = found[:, (j + 2) * width : (j + 3) * width]
-        proj_ref[k, k] = found[:, :width]
-
-    for n in range(ITERS - 1):
-        keep_coeffs(n, left_ref[n, :, :width], coeff_ref[n], shift_ref[n])
-        factors_ref[n] = factor_of(upper_ref[n])
     await_all(late, late_sem)
     packed = jnp.sum(late[...], axis=0) / node_total
     total = jnp.concatenate(
@@ -645,12 +654,13 @@
                 pltpu.VMEM((ITERS,) + small, F32),
                 pltpu.VMEM((2, col_size) + packed, F32),
                 pltpu.VMEM((2, grp_size) + packed, F32),
-                pltpu.VMEM((grp_size * col_size,) + packed, F32),
+                pltpu.VMEM((grp_size,) + packed, F32),
+                pltpu.VMEM((col_size,) + packed, F32),
                 pltpu.VMEM((grp_size * col_size, width // 4, LANES), F32),
                 sems(8 if slots % 8 == 0 else slots),
                 sems(4),
                 sems(2, 4), sems(2, 3), sems(2, 2), sems(2, 2),
-                sems(2), sems(2), sems(2, 2), sems(2, 2), sems(2), sems(2),
+                sems(2), sems(2), sems(2, 2), sems(2, 2), sems(2), sems(2), sems(2),
             ],
             compiler_params=pltpu.CompilerParams(
                 collective_id=0, has_side_effects=True, vmem_limit_bytes=40 * 1024 * 1024

time: 55.4 us -> 55.4 us (level)
  no operation moved by 1% of the time
where the time goes in v6:
time: 55.4 us; the launch traced here: 55.2 us
  Pallas kernels  53.9 us (97%)
  between operations  1.29 us (2%)
    pallas_call x1, Pallas kernels, body(): pl.pallas_call(functools.partial(kernel, grp_size, col_size, node_total),...  53.2 us

profile of v6, /device:TPU:0, one launch (start us, length us, event | category | flops | bytes accessed | tf_op | source)
XLA Modules:
  0.0 55.2 jit_solution(12992339950107816234)
XLA Ops:
  1.3 53.2 %shard_map.76 = (f32[5,16,256]{2,1,0:T(8,128)S(1)}, f32[4,4,16,16]{3,2,1,0:T(8,128)S(1)}, f32[5,16,16]{2,1,0:T(8,128)S(1)}) custom-call(f32[16,256]{1,0:T(8,128)} %start_ref.1, f32[32,256,256]{2,1,0:T(8,128)} %bitcast.5, s32[1,32]{1,0:T(1,128)} %bitcast.6, s32[1,32]{1,0:T(1,128)} %bitcast.7, s32[1]{0:T(128)} %bitcast.4.count_ref), custom_call_target="tpu_custom_call" | custom-call | tf_op jit(solution)/shard_map/pallas_call | solution.py:617
  54.5 0.7 %shard_map.77 = (f32[5,16,256]{2,1,0:T(8,128)}, f32[4,4,16,16]{3,2,1,0:T(8,128)}, f32[5,16,16]{2,1,0:T(8,128)}) custom-call(f32[5,16,256]{2,1,0:T(8,128)S(1)} %get-tuple-element.6.basis, f32[4,4,16,16]{3,2,1,0:T(8,128)S(1)} %get-tuple-element.7.proj, f32[5,16,16]{2,1,0:T(8,128)S(1)} %get-tuple-element.8.factors), custom_call_target="tpu_custom_call" | custom-call | tf_op jit(solution)/shard_map/pallas_call | solution.py:675

commit v7 on v6

--- a/solution.py
+++ b/solution.py
@@ -165,14 +165,14 @@
         bytes_of(buf.at[pl.ds(0, buf.shape[0] - 1)], sems.at[0], sems.at[1]).wait()
 
     col_groups = ((1, grp_size - 1), (grp_size - 1, grp_size))
-    row_groups = ((1, 2), (2, 4), (4, col_size))
+    row_groups = ((1, 4), (4, 6), (6, col_size))
 
     def gather(axis, par, panel, sems, groups):
         me = col if axis == "col" else grp
-        for n, (low_d, high_d) in reversed(list(enumerate(groups))):
+        for n, (low_d, high_d) in enumerate(groups):
 
             def visit(i, carry):
-                d = high_d - 1 - i
+                d = low_d + i
                 target = panel.at[par, me]
                 copy_to(axis, d, lambda peer: u_ref.at[par], target, sems.at[par, 0], sems.at[par, n + 1]).start()
                 return carry
@@ -433,13 +433,13 @@
         red_grp[par, grp] = fold(jnp.where((inner >= width) & (inner < 2 * width), both[width:], both[:width]))
 
     gather("grp", 1, *col_side)
+    gather("col", 1, *row_side)
     inner_products(1, applied)
 
     def step(k, carry):
         par = lax.rem(k + 1, 2)
         block_u, block_r = u_ref[par], stack[1]
         spread("grp", red_grp.at[par], red_grp_sem.at[par], True)
-        gather("col", par, *row_side)
 
         rows_batch(par, [0])
         cols_batch(par, 0, 1)
@@ -453,17 +453,18 @@
         send("col", lambda peer: acc_row.at[peer], got_row.at[par, col], scatter_row_sem.at[par])
         got_row[par, col] = acc_row[col]
         arrive(par, *row_side, 0)
+        cols_batch(par, 1, 3)
         arrive(par, *row_side, 1)
-        cols_batch(par, 1, 3)
+        cols_batch(par, 4, 2)
         arrive(par, *row_side, 2)
-        if col_size <= 8:
-            cols_batch(par, 4, col_size - 4)
-        else:
-            def visit(n, carry):
-                cols_batch(par, 4 * n, 4)
-                return carry
-
-            lax.fori_loop(1, col_size // 4, visit, 0)
+        cols_batch(par, 6, 2)
+
+        def visit(n, carry):
+            cols_batch(par, 4 * n, 4)
+            return carry
+
+        if col_size > 8:
+            lax.fori_loop(2, col_size // 4, visit, 0)
         send("grp", lambda peer: acc_col.at[peer], got_col.at[par, grp], scatter_col_sem.at[par])
         got_col[par, grp] = acc_col[grp]
 
@@ -517,6 +518,7 @@
         @pl.when(k < ITERS - 2)
         def _():
             gather("grp", 1 - par, *col_side)
+            gather("col", 1 - par, *row_side)
 
         inner_products(1 - par, applied)
         lr_ref[...] = fresh_u + sigma * residual

time: 55.4 us -> 53.7 us (0.969)
  Pallas kernels: 53.9 us -> 52.2 us
    pallas_call x1, Pallas kernels: 53.2 us -> 51.5 us  [body(): pl.pallas_call(functools.partial(kernel, grp_size, col_size, node_total),...]
where the time goes in v7:
time: 53.7 us; the launch traced here: 53.5 us
  Pallas kernels  52.2 us (97%)
  between operations  1.29 us (2%)
    pallas_call x1, Pallas kernels, body(): pl.pallas_call(functools.partial(kernel, grp_size, col_size, node_total),...  51.5 us

profile of v7, /device:TPU:0, one launch (start us, length us, event | category | flops | bytes accessed | tf_op | source)
XLA Modules:
  0.0 53.5 jit_solution(9510401178141125324)
XLA Ops:
  1.3 51.5 %shard_map.76 = (f32[5,16,256]{2,1,0:T(8,128)S(1)}, f32[4,4,16,16]{3,2,1,0:T(8,128)S(1)}, f32[5,16,16]{2,1,0:T(8,128)S(1)}) custom-call(f32[16,256]{1,0:T(8,128)} %start_ref.1, f32[32,256,256]{2,1,0:T(8,128)} %bitcast.5, s32[1,32]{1,0:T(1,128)} %bitcast.6, s32[1,32]{1,0:T(1,128)} %bitcast.7, s32[1]{0:T(128)} %bitcast.4.count_ref), custom_call_target="tpu_custom_call" | custom-call | tf_op jit(solution)/shard_map/pallas_call | solution.py:619
  52.8 0.7 %shard_map.77 = (f32[5,16,256]{2,1,0:T(8,128)}, f32[4,4,16,16]{3,2,1,0:T(8,128)}, f32[5,16,16]{2,1,0:T(8,128)}) custom-call(f32[5,16,256]{2,1,0:T(8,128)S(1)} %get-tuple-element.6.basis, f32[4,4,16,16]{3,2,1,0:T(8,128)S(1)} %get-tuple-element.7.proj, f32[5,16,16]{2,1,0:T(8,128)S(1)} %get-tuple-element.8.factors), custom_call_target="tpu_custom_call" | custom-call | tf_op jit(solution)/shard_map/pallas_call | solution.py:677

commit v8 on v7

--- a/solution.py
+++ b/solution.py
@@ -86,7 +86,7 @@
     start_ref, tiles_ref, row_ref, col_ref, count_ref,
     basis_ref, proj_ref, factors_ref,
     raw, merged, high, low, high_t, low_t, rows_v, cols_v, table_v, table,
-    u_ref, lr_ref, stack, lstack, row_panel, col_panel, row_split, col_split,
+    u_ref, lr_ref, stack, lstack, row_panel, col_panel,
     acc_row, acc_col, got_row, got_col, deg_row, deg_col, deg_got_row, deg_got_col,
     degree_ref, sigma_ref, shift_ref, left_ref, upper_ref, coeff_ref, red_col, red_grp, early_grp, early_col, late,
     tile_sem, in_sem, gather_row_sem, gather_col_sem, scatter_row_sem, scatter_col_sem,
@@ -219,43 +219,47 @@
             sems = deg_row_sem
             copy_to("col", d, lambda peer: deg_row.at[r], deg_got_row.at[col], sems.at[0], sems.at[1]).start()
 
-    def halves(panel, par, size, split):
-        for place in range(size):
-            first, second = split_two(panel[par, place])
-            at = pl.ds(place * tile_size, tile_size)
-            split[:width, at] = first
-            split[width : 2 * width, at] = jnp.ones((width, tile_size), BF16)
-            split[2 * width :, at] = second
-
     def combine(total, rest):
         piece = total[:width] + total[2 * width :] + rest[:width]
         return piece, total[width : width + 1] + rest[width : width + 1]
 
-    def rows_of(r):
-        places = [position(r, q) for q in range(grp_size)]
-        left = col_split[...]
-        firsts = jnp.concatenate([high_t[p] for p in places], axis=0)
-        seconds = jnp.concatenate([low[p] for p in places], axis=1)
+    def with_ones(pieces):
+        ones = jnp.ones((width, tile_size), BF16)
+        parts = [split_two(piece) for piece in pieces]
+        return jnp.concatenate([jnp.concatenate([a, ones, b], axis=0) for a, b in parts], axis=1)
+
+    def rows_of(r, left, places):
+        at = [position(r, q) for q in places]
+        firsts = jnp.concatenate([high_t[p] for p in at], axis=0)
+        seconds = jnp.concatenate([low[p] for p in at], axis=1)
         return combine(dot_nn(left, firsts), dot_nt(left[: 2 * width], seconds))
 
-    def cols_of(q):
-        piece, degree = 0.0, 0.0
-        for base in range(0, col_size, CHUNK):
-            left = row_split[:, pl.ds(base * tile_size, CHUNK * tile_size)]
-            places = [position(base + r, q) for r in range(CHUNK)]
-            firsts = jnp.concatenate([high[p] for p in places], axis=0)
-            seconds = jnp.concatenate([low[p] for p in places], axis=0)
-            part, extra = combine(dot_nn(left, firsts), dot_nn(left[: 2 * width], seconds))
-            piece = piece + part
-            degree = degree + extra
-        return piece, degree
+    def cols_of(q, left, places):
+        at = [position(r, q) for r in places]
+        firsts = jnp.concatenate([high[p] for p in at], axis=0)
+        seconds = jnp.concatenate([low[p] for p in at], axis=0)
+        return combine(dot_nn(left, firsts), dot_nn(left[: 2 * width], seconds))
+
+    def first_own():
+        left = with_ones([u_ref[0]])
+
+        def visit(r, carry):
+            acc_row[r], deg_row[r] = rows_of(r, left, [grp])
+            return carry
+
+        lax.fori_loop(0, col_size, visit, 0, unroll=min(col_size, 8))
+        for q in range(grp_size):
+            acc_col[q], deg_col[q] = cols_of(q, left, [col])
 
     def first_rows():
+        places = [flip(grp, d, grp_size) for d in range(1, grp_size)]
+        left = with_ones([col_panel[0, q] for q in places])
+
         def visit(d):
             r = flip(col, d, col_size)
-            piece, degree = rows_of(r)
-            acc_row[r] = piece
-            deg_row[r] = degree
+            piece, degree = rows_of(r, left, places)
+            acc_row[r] = acc_row[r] + piece
+            deg_row[r] = deg_row[r] + degree
 
         def go(ds):
             for d in ds:
@@ -278,11 +282,20 @@
         deg_got_row[col] = deg_row[col]
 
     def first_cols():
-        for d in range(grp_size - 1, -1, -1):
-            q = flip(grp, d, grp_size)
-            piece, degree = cols_of(q)
-            acc_col[q] = piece
-            deg_col[q] = degree
+        def batch(places):
+            left = with_ones([row_panel[0, r] for r in places])
+            for q in range(grp_size):
+                piece, degree = cols_of(q, left, places)
+                acc_col[q] = acc_col[q] + piece
+                deg_col[q] = deg_col[q] + degree
+
+        def visit(n, carry):
+            batch([flip(col, n * CHUNK + i, col_size) for i in range(CHUNK)])
+            return carry
+
+        batch([flip(col, i, col_size) for i in range(1, CHUNK)])
+        if col_size > CHUNK:
+            lax.fori_loop(1, col_size // CHUNK, visit, 0)
         send("grp", lambda peer: acc_col.at[peer], got_col.at[0, grp], scatter_col_sem.at[0])
         got_col[0, grp] = acc_col[grp]
         send("grp", lambda peer: deg_col.at[peer], deg_got_col.at[grp], deg_col_sem)
@@ -369,8 +382,6 @@
     start = u_ref[0]
     stack[0] = start
     stack[1] = start
-    row_panel[0, col] = start
-    col_panel[0, grp] = start
     pl.semaphore_wait(barrier, everyone - 1)
     gather("grp", 0, *col_side)
     gather("col", 0, *row_side)
@@ -393,13 +404,12 @@
 
     lax.fori_loop(0, loads_of, merge, 0)
 
+    first_own()
     for n in range(len(col_groups)):
         arrive(0, *col_side, n)
-    halves(col_panel, 0, grp_size, col_split)
     first_rows()
     for n in range(len(row_groups)):
         arrive(0, *row_side, n)
-    halves(row_panel, 0, col_size, row_split)
     first_cols()
 
     def turn(s, carry):
@@ -432,22 +442,24 @@
         inner = lax.rem(lane, 4 * width)
         red_grp[par, grp] = fold(jnp.where((inner >= width) & (inner < 2 * width), both[width:], both[:width]))
 
-    gather("grp", 1, *col_side)
-    gather("col", 1, *row_side)
+    def depart(par):
+        spread("grp", red_grp.at[par], red_grp_sem.at[par], True)
+        gather("grp", par, *col_side)
+        gather("col", par, *row_side)
+
     inner_products(1, applied)
+    depart(1)
 
     def step(k, carry):
         par = lax.rem(k + 1, 2)
         block_u, block_r = u_ref[par], stack[1]
-        spread("grp", red_grp.at[par], red_grp_sem.at[par], True)
-
         rows_batch(par, [0])
         cols_batch(par, 0, 1)
         arrive(par, *col_side, 0)
-        rows_batch(par, list(range(1, grp_size - 1)))
         spread("grp", red_grp.at[par], red_grp_sem.at[par], False)
         red_col[par, col] = jnp.sum(red_grp[par], axis=0)
         spread("col", red_col.at[par], red_col_sem.at[par], True)
+        rows_batch(par, list(range(1, grp_size - 1)))
         arrive(par, *col_side, 1)
         rows_batch(par, [grp_size - 1])
         send("col", lambda peer: acc_row.at[peer], got_row.at[par, col], scatter_row_sem.at[par])
@@ -512,16 +524,22 @@
         shift_ref[k] = before[:, :LANES]
 
         applied = collect(par, False) - known
-        fresh_u = dot_nn(left, applied, HIGHEST)
-        u_ref[1 - par] = fresh_u
+
+        def renew():
+            block_u = dot_nn(left, applied, HIGHEST)
+            u_ref[1 - par] = block_u
+            return block_u
 
         @pl.when(k < ITERS - 2)
         def _():
-            gather("grp", 1 - par, *col_side)
-            gather("col", 1 - par, *row_side)
-
-        inner_products(1 - par, applied)
-        lr_ref[...] = fresh_u + sigma * residual
+            lr_ref[...] = renew() + sigma * residual
+            inner_products(1 - par, applied)
+            depart(1 - par)
+
+        @pl.when(k == ITERS - 2)
+        def _():
+            renew()
+
         return carry
 
     lax.fori_loop(0, ITERS - 1, step, 0)
@@ -638,8 +656,6 @@
                 pltpu.VMEM((places,) + block, F32),
                 pltpu.VMEM((2, col_size) + block, F32),
                 pltpu.VMEM((2, grp_size) + block, F32),
-                pltpu.VMEM((3 * width, col_size * tile_size), BF16),
-                pltpu.VMEM((3 * width, grp_size * tile_size), BF16),
                 pltpu.VMEM((col_size,) + block, F32),
                 pltpu.VMEM((grp_size,) + block, F32),
                 pltpu.VMEM((2, col_size) + block, F32),

time: 53.7 us -> 53.8 us (level)
  no operation moved by 1% of the time
where the time goes in v8:
time: 53.8 us; the launch traced here: 53.6 us
  Pallas kernels  52.3 us (97%)
  between operations  1.29 us (2%)
    pallas_call x1, Pallas kernels, body(): pl.pallas_call(functools.partial(kernel, grp_size, col_size, node_total),...  51.6 us

profile of v8, /device:TPU:0, one launch (start us, length us, event | category | flops | bytes accessed | tf_op | source)
XLA Modules:
  0.0 53.6 jit_solution(804186274968718267)
XLA Ops:
  1.3 51.6 %shard_map.76 = (f32[5,16,256]{2,1,0:T(8,128)S(1)}, f32[4,4,16,16]{3,2,1,0:T(8,128)S(1)}, f32[5,16,16]{2,1,0:T(8,128)S(1)}) custom-call(f32[16,256]{1,0:T(8,128)} %start_ref.1, f32[32,256,256]{2,1,0:T(8,128)} %bitcast.5, s32[1,32]{1,0:T(1,128)} %bitcast.6, s32[1,32]{1,0:T(1,128)} %bitcast.7, s32[1]{0:T(128)} %bitcast.4.count_ref), custom_call_target="tpu_custom_call" | custom-call | tf_op jit(solution)/shard_map/pallas_call | solution.py:637
  52.9 0.7 %shard_map.77 = (f32[5,16,256]{2,1,0:T(8,128)}, f32[4,4,16,16]{3,2,1,0:T(8,128)}, f32[5,16,16]{2,1,0:T(8,128)}) custom-call(f32[5,16,256]{2,1,0:T(8,128)S(1)} %get-tuple-element.6.basis, f32[4,4,16,16]{3,2,1,0:T(8,128)S(1)} %get-tuple-element.7.proj, f32[5,16,16]{2,1,0:T(8,128)S(1)} %get-tuple-element.8.factors), custom_call_target="tpu_custom_call" | custom-call | tf_op jit(solution)/shard_map/pallas_call | solution.py:693

commit v9 on v8

--- a/solution.py
+++ b/solution.py
@@ -441,14 +441,14 @@
         both = dot_nt(jnp.concatenate([block_v, stack[1]], axis=0), block, HIGHEST)
         inner = lax.rem(lane, 4 * width)
         red_grp[par, grp] = fold(jnp.where((inner >= width) & (inner < 2 * width), both[width:], both[:width]))
+        spread("grp", red_grp.at[par], red_grp_sem.at[par], True)
 
     def depart(par):
-        spread("grp", red_grp.at[par], red_grp_sem.at[par], True)
         gather("grp", par, *col_side)
         gather("col", par, *row_side)
 
+    depart(1)
     inner_products(1, applied)
-    depart(1)
 
     def step(k, carry):
         par = lax.rem(k + 1, 2)
@@ -456,10 +456,10 @@
         rows_batch(par, [0])
         cols_batch(par, 0, 1)
         arrive(par, *col_side, 0)
+        rows_batch(par, list(range(1, grp_size - 1)))
         spread("grp", red_grp.at[par], red_grp_sem.at[par], False)
         red_col[par, col] = jnp.sum(red_grp[par], axis=0)
         spread("col", red_col.at[par], red_col_sem.at[par], True)
-        rows_batch(par, list(range(1, grp_size - 1)))
         arrive(par, *col_side, 1)
         rows_batch(par, [grp_size - 1])
         send("col", lambda peer: acc_row.at[peer], got_row.at[par, col], scatter_row_sem.at[par])
@@ -532,9 +532,10 @@
 
         @pl.when(k < ITERS - 2)
         def _():
-            lr_ref[...] = renew() + sigma * residual
+            block_u = renew()
+            depart(1 - par)
             inner_products(1 - par, applied)
-            depart(1 - par)
+            lr_ref[...] = block_u + sigma * residual
 
         @pl.when(k == ITERS - 2)
         def _():

time: 53.8 us -> 53.2 us (0.989)
  Pallas kernels: 52.3 us -> 51.7 us
    pallas_call x1, Pallas kernels: 51.6 us -> 51 us  [body(): pl.pallas_call(functools.partial(kernel, grp_size, col_size, node_total),...]
where the time goes in v9:
time: 53.2 us; the launch traced here: 53 us
  Pallas kernels  51.7 us (97%)
  between operations  1.29 us (2%)
    pallas_call x1, Pallas kernels, body(): pl.pallas_call(functools.partial(kernel, grp_size, col_size, node_total),...  51 us

profile of v9, /device:TPU:0, one launch (start us, length us, event | category | flops | bytes accessed | tf_op | source)
XLA Modules:
  0.0 53.0 jit_solution(1120708724019191788)
XLA Ops:
  1.3 51.0 %shard_map.76 = (f32[5,16,256]{2,1,0:T(8,128)S(1)}, f32[4,4,16,16]{3,2,1,0:T(8,128)S(1)}, f32[5,16,16]{2,1,0:T(8,128)S(1)}) custom-call(f32[16,256]{1,0:T(8,128)} %start_ref.1, f32[32,256,256]{2,1,0:T(8,128)} %bitcast.5, s32[1,32]{1,0:T(1,128)} %bitcast.6, s32[1,32]{1,0:T(1,128)} %bitcast.7, s32[1]{0:T(128)} %bitcast.4.count_ref), custom_call_target="tpu_custom_call" | custom-call | tf_op jit(solution)/shard_map/pallas_call | solution.py:638
  52.3 0.7 %shard_map.77 = (f32[5,16,256]{2,1,0:T(8,128)}, f32[4,4,16,16]{3,2,1,0:T(8,128)}, f32[5,16,16]{2,1,0:T(8,128)}) custom-call(f32[5,16,256]{2,1,0:T(8,128)S(1)} %get-tuple-element.6.basis, f32[4,4,16,16]{3,2,1,0:T(8,128)S(1)} %get-tuple-element.7.proj, f32[5,16,16]{2,1,0:T(8,128)S(1)} %get-tuple-element.8.factors), custom_call_target="tpu_custom_call" | custom-call | tf_op jit(solution)/shard_map/pallas_call | solution.py:694

commit v10 on v9

--- a/solution.py
+++ b/solution.py
@@ -568,6 +568,11 @@
     for n in range(ITERS - 1):
         keep_coeffs(n, left_ref[n, :, :width], coeff_ref[n], shift_ref[n])
         factors_ref[n] = factor_of(upper_ref[n])
+    await_all(late, late_sem)
+    packed = jnp.sum(late[...], axis=0) / node_total
+    newer = jnp.concatenate(
+        [packed] + [pltpu.roll(packed, LANES - n * 2 * width, 1) for n in range(1, 4)], axis=0
+    )
     spread("col", early_col, early_col_sem, False)
     total = unfold(jnp.sum(early_col[...], axis=0) / node_total)
     upper, inverse = factorize(total)
@@ -578,15 +583,10 @@
     factors_ref[k] = factor_of(upper)
     older = jnp.where((lane >= 2 * width) & (lane < 5 * width), total, 0.0)
     pad = jnp.concatenate([inverse, jnp.zeros((LANES - width, LANES), F32)], axis=0)[:, :width]
-    await_all(late, late_sem)
-    packed = jnp.sum(late[...], axis=0) / node_total
-    total = jnp.concatenate(
-        [packed] + [pltpu.roll(packed, LANES - n * 2 * width, 1) for n in range(1, 4)], axis=0
-    )
-    coeffs = dot_nt(total[:, :width], pad, HIGHEST) + older
+    coeffs = dot_nt(newer[:, :width], pad, HIGHEST) + older
     middle = jnp.zeros((width, LANES), F32)
     beside = jnp.concatenate([middle, coeffs] + [middle] * (LANES // width - 2), axis=0)
-    gram = total - dot_nt(coeffs, beside, HIGHEST)
+    gram = newer - dot_nt(coeffs, beside, HIGHEST)
     rest = block_u - dot_nn(coeffs, stack[...].reshape(LANES, tile_size), HIGHEST)
     upper, inverse = factorize(gram)
     basis_ref[ITERS] = dot_nn(inverse[:, :width], rest, HIGHEST)

time: 53.2 us -> 53 us (level)
  no operation moved by 1% of the time
where the time goes in v10:
time: 53 us; the launch traced here: 52.8 us
  Pallas kernels  51.5 us (97%)
  between operations  1.29 us (2%)
    pallas_call x1, Pallas kernels, body(): pl.pallas_call(functools.partial(kernel, grp_size, col_size, node_total),...  50.8 us

profile of v10, /device:TPU:0, one launch (start us, length us, event | category | flops | bytes accessed | tf_op | source)
XLA Modules:
  0.0 52.8 jit_solution(12353054700498529705)
XLA Ops:
  1.3 50.8 %shard_map.76 = (f32[5,16,256]{2,1,0:T(8,128)S(1)}, f32[4,4,16,16]{3,2,1,0:T(8,128)S(1)}, f32[5,16,16]{2,1,0:T(8,128)S(1)}) custom-call(f32[16,256]{1,0:T(8,128)} %start_ref.1, f32[32,256,256]{2,1,0:T(8,128)} %bitcast.5, s32[1,32]{1,0:T(1,128)} %bitcast.6, s32[1,32]{1,0:T(1,128)} %bitcast.7, s32[1]{0:T(128)} %bitcast.4.count_ref), custom_call_target="tpu_custom_call" | custom-call | tf_op jit(solution)/shard_map/pallas_call | solution.py:638
  52.1 0.7 %shard_map.77 = (f32[5,16,256]{2,1,0:T(8,128)}, f32[4,4,16,16]{3,2,1,0:T(8,128)}, f32[5,16,16]{2,1,0:T(8,128)}) custom-call(f32[5,16,256]{2,1,0:T(8,128)S(1)} %get-tuple-element.6.basis, f32[4,4,16,16]{3,2,1,0:T(8,128)S(1)} %get-tuple-element.7.proj, f32[5,16,16]{2,1,0:T(8,128)S(1)} %get-tuple-element.8.factors), custom_call_target="tpu_custom_call" | custom-call | tf_op jit(solution)/shard_map/pallas_call | solution.py:694
